TPU v7x, 128 devices: a whole 4x4x4 slice. The times are simulated.
128 devices in a mesh: row: 16 (over x, z), col: 8 (over y, core).
Axes of the slice: x: 4, y: 4, z: 4, core: 2. Of those that a mesh axis runs over, the one named last changes fastest.
Arguments:
- front: float32 [9216, 9216], P('row', 'col')
- child_tiles: float32 [16384, 4096], P(('row', 'col')), may hold values from -0.4375 to 0.4375
- tile_target: int32 [16384], P(('row', 'col')), may hold values from 0 to 20735, as said below
- tile_count: int32 [512], P(('row', 'col')), may hold values from 24 to 32
- probe: float32 [9216, 512], P('col'), may hold values from -1.75 to 1.75
Outputs:
- panel_factor: float32 [9216, 1024], P('row', 'col')
- sketch: float32 [9216, 512], P('row', 'col')
Inputs may be any that keep to these rules, and one draw needn't show every extreme that they name: `tile_target`: among the 128 slots of one device, live or not, each counted once at its target tile and once at the mirrored tile, at most 2 placements fall inside the block of the front held by any one device.
All inputs are finite; a program needn't handle non-finite values.
Results may differ from a plain program's by a relative error of at most 0.00015.
Values sent between devices are 32-bit elements; how exact they have to be, the bound alone decides.
A program may use at most 128 MiB of HBM per device.

v0:
```python
import jax
import jax.numpy as jnp
from jax import lax
from jax.sharding import PartitionSpec as P

NB = 512
PANELS = 2
TB = 64
SLOTS = 32


HIGH = lax.Precision.HIGHEST


def in_blocks(value, dim, size):
    before, after = (value.shape[:dim], value.shape[dim + 1 :])
    return jnp.moveaxis(value.reshape(*before, size, -1, *after), dim, 0)


def joined_along(tiles, dim):
    lengths = list(tiles.shape[1:])
    lengths[dim] *= tiles.shape[0]
    return jnp.moveaxis(tiles, 0, dim).reshape(lengths)


def one_exchange(value, axis, axes, splits, concats):
    sizes = [lax.axis_size(a) for a in axes]
    tiles = in_blocks(value, splits[0], sizes[0])
    tiles = jnp.moveaxis(in_blocks(tiles, splits[1] + 1, sizes[1]), 0, 1)
    inside = tiles.shape[2:]
    tiles = tiles.reshape(-1, *inside)
    tiles = lax.all_to_all(tiles, axis, split_axis=0, concat_axis=0, tiled=True)
    tiles = joined_along(tiles.reshape(*sizes, *inside), concats[0] + 1)
    return joined_along(tiles, concats[1])


def filled_up(lines, size):
    spare = -lines.shape[0] % size
    if not spare:
        return lines
    return jnp.concatenate([lines, jnp.zeros((spare, *lines.shape[1:]), lines.dtype)])


def from_root(value, axis, root):
    lines = jnp.where(lax.axis_index(axis) == root, value, jnp.zeros_like(value)).reshape(
        -1, *value.shape[1:][-1:]
    )
    padded = filled_up(lines, lax.axis_size(axis))
    own = lax.psum_scatter(padded, axis, scatter_dimension=0, tiled=True)
    return lax.all_gather(own, axis, axis=0, tiled=True)[: len(lines)].reshape(value.shape)


def broadcast(value, axis, root):
    mine = lax.axis_index(axis) == root
    return lax.psum(jnp.where(mine, value, jnp.zeros_like(value)), axis)


def sum_at_owner(value, axis, dim):
    tiles = in_blocks(value, dim, lax.axis_size(axis))
    arrived = lax.all_to_all(tiles, axis, split_axis=0, concat_axis=0, tiled=True)
    return arrived.sum(axis=0)


def per_device(front, child_tiles, tile_target, tile_count, probe):
    row_count = lax.axis_size("row")
    col_count = lax.axis_size("col")
    devices = row_count * col_count
    local_rows, local_cols = front.shape
    tile_rows = local_rows // TB
    tile_cols = local_cols // TB
    grid = tile_cols * col_count
    local_tiles = tile_rows * tile_cols
    held = child_tiles.shape[0]
    capacity = 2 * max(1, (held + devices - 1) // devices)
    slot_index = jnp.arange(held, dtype=jnp.int32)
    live_once = slot_index % SLOTS < tile_count[slot_index // SLOTS]
    live = jnp.concatenate([live_once, live_once])
    mirrored = child_tiles.reshape(held, TB, TB).transpose(0, 2, 1).reshape(held, TB * TB)
    placements = jnp.concatenate([child_tiles, mirrored], axis=0)
    first_row = tile_target // grid
    first_col = tile_target % grid
    target_row = jnp.concatenate([first_row, first_col])
    target_col = jnp.concatenate([first_col, first_row])
    owner = target_row // tile_rows * col_count + target_col // tile_cols
    place = target_row % tile_rows * tile_cols + target_col % tile_cols
    onehot = (
        (owner[:, None] == jnp.arange(devices, dtype=jnp.int32)[None, :]) & live[:, None]
    ).astype(jnp.int32)
    earlier = jnp.cumsum(onehot, axis=0) - onehot
    rank = jnp.sum(earlier * onehot, axis=1)
    slot = jnp.where(live, owner * capacity + rank, devices * capacity)
    outgoing = (
        jnp.zeros((devices * capacity + 1, TB * TB), jnp.float32).at[slot].set(placements)[:-1]
    )
    where_to = jnp.full((devices * capacity + 1,), local_tiles, jnp.int32).at[slot].set(place)[:-1]
    shaped = (
        outgoing.reshape(row_count, col_count * capacity, TB * TB),
        where_to.reshape(row_count, col_count * capacity),
    )
    incoming, landing = (
        one_exchange(shaped[0], ("row", "col"), ("row", "col"), (0, 1), (0, 1)),
        one_exchange(shaped[1], ("row", "col"), ("row", "col"), (0, 1), (0, 1)),
    )
    incoming = incoming.reshape(-1, TB * TB)
    landing = landing.reshape(-1)
    extend = (
        jnp.zeros((local_tiles + 1, TB * TB), jnp.float32).at[landing].add(incoming)[:local_tiles]
    )
    extend = (
        extend.reshape(tile_rows, tile_cols, TB, TB)
        .transpose(0, 2, 1, 3)
        .reshape(local_rows, local_cols)
    )
    matrix = front + extend
    row_start = lax.axis_index("row") * local_rows
    col_start = lax.axis_index("col") * local_cols
    global_rows = row_start + jnp.arange(local_rows, dtype=jnp.int32)
    group = row_count // col_count
    margin = jnp.zeros((NB, NB), jnp.float32)
    factor_parts = []
    for k in range(PANELS):
        low = k * NB
        high = low + NB
        owner_col = low // local_cols
        offset = low % local_cols
        panel = from_root(matrix[:, offset : offset + NB], "col", owner_col)
        padded = jnp.concatenate([margin, panel, margin], axis=0)
        begin = jnp.clip(low - row_start + NB, 0, local_rows + NB)
        piece = lax.dynamic_slice_in_dim(padded, begin, NB, 0)
        diag_block = lax.psum(piece, "row")
        chol = jnp.linalg.cholesky(0.5 * (diag_block + diag_block.T))
        solved = jax.scipy.linalg.solve_triangular(chol, panel.T, lower=True).T
        factor_parts.append(jnp.where((global_rows >= low)[:, None], solved, 0.0))
        trail = jnp.where((global_rows >= high)[:, None], solved, 0.0)
        column_owner = lax.axis_index("col") * group
        pieces = [broadcast(trail, "row", column_owner + member) for member in range(group)]
        across = jnp.concatenate(pieces, axis=0)
        matrix = matrix - jnp.dot(trail, across.T, precision=HIGH)
    start = PANELS * NB
    global_cols = col_start + jnp.arange(local_cols, dtype=jnp.int32)
    weighted = jnp.where((global_cols >= start)[:, None], probe, 0.0)
    shares = sum_at_owner(
        lax.dot_general(weighted, matrix, (((0,), (1,)), ((), ())), precision=HIGH), "col", 0
    )
    sketch = jnp.where((global_rows >= start)[:, None], shares.T, 0.0)
    all_panels = jnp.concatenate(factor_parts, axis=1)
    width = all_panels.shape[1] // col_count
    panel_factor = lax.dynamic_slice_in_dim(all_panels, lax.axis_index("col") * width, width, 1)
    return (panel_factor, sketch)


def solution(mesh):
    return jax.shard_map(
        per_device,
        mesh=mesh,
        in_specs=(
            P("row", "col"),
            P(("row", "col"), None),
            P(("row", "col")),
            P(("row", "col")),
            P("col", None),
        ),
        out_specs=(P("row", "col"), P("row", "col")),
        check_vma=False,
    )
```

profile of v0, /device:TPU:9, one launch (start us, length us, event | category | flops | bytes accessed | tf_op | source)
XLA Modules:
  0.0 1001.6 jit_solution(17757820655012956910)
XLA Ops:
  17.6 10.7 %all-to-all-start = ((s32[128,1,2]{2,1,0:T(1,128)}), s32[128,1,2]{2,1,0:T(1,128)S(1)}, u32[]{:S(2)}, u32[]{:S(2)}) async-start(s32[128,1,2]{2,1,0:T(1,128)} %bitcast.16), calls=%async_computation | async-start | bytes 131072 | tf_op jit(solution)/shard_map/all_to_all | solution.py:32
  33.7 5.7 copy.35
  39.4 6.8 scatter_custom_fusion.1
  46.1 4.6 slice.127
  50.8 5.8 reshape_transpose_transpose_reshape_reshape_reshape.7
  56.6 10.2 %all-to-all-start.1 = ((f32[128,1,2,4096]{3,2,1,0:T(2,128)}), f32[128,1,2,4096]{3,2,1,0:T(2,128)}, u32[]{:S(2)}, u32[]{:S(2)}) async-start(f32[128,1,2,4096]{3,2,1,0:T(2,128)} %bitcast.188), calls=%async_computation.1 | async-start | bytes 8388608 | tf_op jit(solution)/shard_map/all_to_all | solution.py:32
  67.2 50.7 %all-to-all-done.1 = f32[128,1,2,4096]{3,2,1,0:T(2,128)} async-done(((f32[128,1,2,4096]{3,2,1,0:T(2,128)}), f32[128,1,2,4096]{3,2,1,0:T(2,128)}, u32[]{:S(2)}, u32[]{:S(2)}) %all-to-all-start.1) | async-done | bytes 4194336 | tf_op jit(solution)/shard_map/all_to_all | solution.py:32
  117.9 6.0 reshape.543
  124.0 8.4 scatter_custom_fusion.2
  132.3 4.4 reshape.487
  136.8 8.6 copy.37
  145.3 6.2 reshape.488
  151.5 2.8 add.248
  155.6 27.3 %reduce-scatter.3.cloned.1.call-done = f32[72,512]{1,0:T(8,128)} async-done(((f32[576,512]{1,0:T(8,128)}), f32[72,512]{1,0:T(8,128)}) %reduce-scatter.3.cloned.1.call-update) | async-done | bytes 147472 | tf_op jit(solution)/shard_map/reduce_scatter | solution.py:49
  183.0 26.5 %all-gather.3.cloned.1.call-done = f32[576,512]{1,0:T(8,128)} async-done(((f32[72,512]{1,0:T(8,128)}), f32[576,512]{1,0:T(8,128)}) %all-gather.3.cloned.1.call-update) | async-done | bytes 1179664 | tf_op jit(solution)/shard_map/all_gather | solution.py:50
  210.6 2.9 fusion.17
  214.0 86.5 %all-reduce.8.cloned.1.call-done = f32[512,512]{1,0:T(8,128)} async-done(((f32[512,512]{1,0:T(8,128)}), f32[512,512]{1,0:T(8,128)}) %all-reduce.8.cloned.1.call-update) | async-done | bytes 1048592 | tf_op jit(solution)/shard_map/psum | solution.py:130
  303.1 2.7 fusion.20
  305.8 2.6 copy.39
  311.2 11.7 %cholesky.286 = f32[128,128]{1,0:T(8,128)S(1)} custom-call(f32[128,128]{1,0:T(8,128)S(1)} %cholesky.426), custom_call_target="Cholesky" | custom-call | tf_op jit(solution)/shard_map/jit(cholesky)/cholesky | solution.py:131
  324.1 9.8 custom-call.27
  337.1 11.7 %cholesky.305 = f32[128,128]{1,0:T(8,128)S(1)} custom-call(f32[128,128]{1,0:T(8,128)S(1)} %cholesky.430), custom_call_target="Cholesky" | custom-call | tf_op jit(solution)/shard_map/jit(cholesky)/cholesky | solution.py:131
  349.5 10.0 custom-call.28
  361.8 11.7 %cholesky.326 = f32[128,128]{1,0:T(8,128)S(1)} custom-call(f32[128,128]{1,0:T(8,128)S(1)} %cholesky.435), custom_call_target="Cholesky" | custom-call | tf_op jit(solution)/shard_map/jit(cholesky)/cholesky | solution.py:131
  374.8 9.8 custom-call.29
  386.9 12.1 %cholesky.343 = f32[128,128]{1,0:T(8,128)S(1)} custom-call(f32[128,128]{1,0:T(8,128)S(1)} %convolution_subtract_fusion.13), custom_call_target="Cholesky" | custom-call | tf_op jit(solution)/shard_map/jit(cholesky)/cholesky | solution.py:131
  405.9 11.9 %while.4 = (s32[]{:T(128)}, f32[512,512]{1,0:T(8,128)}, s32[4,2]{0,1:T(2,128)S(1)}, f32[4,128,128]{2,1,0:T(8,128)S(1)}, s32[]{:T(128)}) while((s32[]{:T(128)}, f32[512,512]{1,0:T(8,128)}, s32[4,2]{0,1:T(2,128)S(1)}, f32[4,128,128]{2,1,0:T(8,128)S(1)}, s32[]{:T(128)}) %tuple.68), condition=%wide.while_cond, body=%wide.while_body.sunk | while | flops 2 | bytes 131181 | solution.py:132
  417.8 39.3 %custom-call.30 = f32[4,128,128]{1,2,0:T(8,128)S(1)} custom-call(f32[4,128,128]{2,1,0:T(8,128)S(1)} %get-tuple-element.18), custom_call_target="InvertDiagBlocksLowerTriangular" | custom-call | tf_op jit(solution)/shard_map/jit(_solve_triangular)/triangular_solve | solution.py:132
  468.6 91.7 %all-reduce.14.cloned.1.call-done = (f32[576,512]{1,0:T(8,128)}, f32[576,512]{1,0:T(8,128)}) async-done(((f32[576,512]{1,0:T(8,128)}, f32[576,512]{1,0:T(8,128)}), (f32[576,512]{1,0:T(8,128)}, f32[576,512]{1,0:T(8,128)})) %all-reduce.14.cloned.1.call-update) | async-done | bytes 2359312 | tf_op jit(solution)/shard_map/psum | solution.py:55
  560.3 6.9 convolution_subtract_fusion.1
  569.9 29.4 %reduce-scatter.5.cloned.1.call-done = f32[72,512]{1,0:T(8,128)} async-done(((f32[576,512]{1,0:T(8,128)}), f32[72,512]{1,0:T(8,128)}) %reduce-scatter.5.cloned.1.call-update) | async-done | bytes 147472 | tf_op jit(solution)/shard_map/reduce_scatter | solution.py:49
  599.4 26.3 %all-gather.5.cloned.1.call-done = f32[576,512]{1,0:T(8,128)} async-done(((f32[72,512]{1,0:T(8,128)}), f32[576,512]{1,0:T(8,128)}) %all-gather.5.cloned.1.call-update) | async-done | bytes 1179664 | tf_op jit(solution)/shard_map/all_gather | solution.py:50
  625.7 2.6 fusion.15
  628.5 87.8 %all-reduce.10.cloned.1.call-done = f32[512,512]{1,0:T(8,128)} async-done(((f32[512,512]{1,0:T(8,128)}), f32[512,512]{1,0:T(8,128)}) %all-reduce.10.cloned.1.call-update) | async-done | bytes 1048592 | tf_op jit(solution)/shard_map/psum | solution.py:130
  719.2 11.7 %cholesky.358 = f32[128,128]{1,0:T(8,128)S(1)} custom-call(f32[128,128]{1,0:T(8,128)S(1)} %cholesky.439), custom_call_target="Cholesky" | custom-call | tf_op jit(solution)/shard_map/jit(cholesky)/cholesky | solution.py:131
  731.1 9.8 custom-call.31
  741.6 11.7 %cholesky.377 = f32[128,128]{1,0:T(8,128)S(1)} custom-call(f32[128,128]{1,0:T(8,128)S(1)} %cholesky.443), custom_call_target="Cholesky" | custom-call | tf_op jit(solution)/shard_map/jit(cholesky)/cholesky | solution.py:131
  754.6 10.2 %custom-call.32 = f32[1,128,128]{1,2,0:T(8,128)S(1)} custom-call(f32[1,128,128]{2,1,0:T(8,128)S(1)} %get-tuple-element.58), custom_call_target="InvertDiagBlocksLowerTriangular" | custom-call | tf_op jit(solution)/shard_map/jit(cholesky)/cholesky | solution.py:131
  765.4 11.7 %cholesky.398 = f32[128,128]{1,0:T(8,128)S(1)} custom-call(f32[128,128]{1,0:T(8,128)S(1)} %cholesky.448), custom_call_target="Cholesky" | custom-call | tf_op jit(solution)/shard_map/jit(cholesky)/cholesky | solution.py:131
  777.8 9.8 custom-call.33
  788.2 11.9 %cholesky.415 = f32[128,128]{1,0:T(8,128)S(1)} custom-call(f32[128,128]{1,0:T(8,128)S(1)} %convolution_subtract_fusion.12), custom_call_target="Cholesky" | custom-call | tf_op jit(solution)/shard_map/jit(cholesky)/cholesky | solution.py:131
  803.5 7.7 while.5
  811.2 39.3 %custom-call.34 = f32[4,128,128]{1,2,0:T(8,128)S(1)} custom-call(f32[4,128,128]{2,1,0:T(8,128)S(1)} %get-tuple-element.19), custom_call_target="InvertDiagBlocksLowerTriangular" | custom-call | tf_op jit(solution)/shard_map/jit(_solve_triangular)/triangular_solve | solution.py:132
  858.9 91.8 %all-reduce.12.cloned.1.call-done = (f32[576,512]{1,0:T(8,128)}, f32[576,512]{1,0:T(8,128)}) async-done(((f32[576,512]{1,0:T(8,128)}, f32[576,512]{1,0:T(8,128)}), (f32[576,512]{1,0:T(8,128)}, f32[576,512]{1,0:T(8,128)})) %all-reduce.12.cloned.1.call-update) | async-done | bytes 2359312 | tf_op jit(solution)/shard_map/psum | solution.py:55
  950.7 7.0 convolution_subtract_fusion
  957.7 12.7 %fusion.6 = f32[512,576]{1,0:T(8,128)} fusion(f32[576,1152]{1,0:T(8,128)S(1)} %convolution_subtract_fusion, f32[1152,512]{1,0:T(8,128)S(1)} %copy-done.12, pred[1152]{0:T(1024)(128)(4,1)S(1)} %add_compare_fusion), kind=kOutput, calls=%fused_computation.24 | convolution fusion | flops 4077453312 | bytes 6194304 | tf_op jit(solution)/shard_map/dot_general | solution.py:143
  970.4 6.7 all-to-all-start.2
  977.8 15.9 %all-to-all-done.2 = f32[8,64,576]{2,1,0:T(8,128)S(1)} async-done(((f32[8,64,576]{2,1,0:T(8,128)}), f32[8,64,576]{2,1,0:T(8,128)S(1)}, u32[]{:S(2)}, u32[]{:S(2)}) %all-to-all-start.2) | async-done | bytes 1179680 | tf_op jit(solution)/shard_map/all_to_all | solution.py:60
  (171 shorter events, 91.0 us)
Async XLA Ops:
  17.6 39.0 %all-to-all-start = ((s32[128,1,2]{2,1,0:T(1,128)}), s32[128,1,2]{2,1,0:T(1,128)S(1)}, u32[]{:S(2)}, u32[]{:S(2)}) async-start(s32[128,1,2]{2,1,0:T(1,128)} %bitcast.16), calls=%async_computation | async-start | bytes 131072 | tf_op jit(solution)/shard_map/all_to_all | solution.py:32
  56.6 61.3 %all-to-all-start.1 = ((f32[128,1,2,4096]{3,2,1,0:T(2,128)}), f32[128,1,2,4096]{3,2,1,0:T(2,128)}, u32[]{:S(2)}, u32[]{:S(2)}) async-start(f32[128,1,2,4096]{3,2,1,0:T(2,128)} %bitcast.188), calls=%async_computation.1 | async-start | bytes 8388608 | tf_op jit(solution)/shard_map/all_to_all | solution.py:32
  66.8 116.1 %reduce-scatter.3.cloned.1.call-start = ((), (), s32[]{:S(2)}) async-start(), calls=%async_computation.5 | async-start | bytes 1327104 | tf_op jit(solution)/shard_map/reduce_scatter | solution.py:49
  155.5 54.0 %all-gather.3.cloned.1.call-start = ((), (), s32[]{:S(2)}) async-start(), calls=%async_computation.6 | async-start | bytes 1327104 | tf_op jit(solution)/shard_map/all_gather | solution.py:50
  182.9 117.6 %all-reduce.8.cloned.1.call-start = ((), (), s32[]{:S(2)}) async-start(), calls=%async_computation.7 | async-start | bytes 2097152 | tf_op jit(solution)/shard_map/psum | solution.py:130
  209.6 1.0 copy-start.2
  213.6 346.7 %all-reduce.14.cloned.1.call-start = ((), (), s32[]{:S(2)}) async-start(), calls=%async_computation.12 | async-start | bytes 4718592 | tf_op jit(solution)/shard_map/psum | solution.py:55
  310.2 1.0 copy-start.9
  457.2 3.3 copy-start.13
  457.2 3.3 copy-start.4
  466.4 2.1 copy-start.11
  468.5 130.8 %reduce-scatter.5.cloned.1.call-start = ((), (), s32[]{:S(2)}) async-start(), calls=%async_computation.8 | async-start | bytes 1327104 | tf_op jit(solution)/shard_map/reduce_scatter | solution.py:49
  567.1 1.5 copy-start
  569.8 55.9 %copy-start.3 = (f32[512,512]{1,0:T(8,128)S(1)}, f32[512,512]{1,0:T(8,128)}, u32[]{:S(2)}) copy-start(f32[512,512]{1,0:T(8,128)} %copy-done.2) | copy-start | bytes 3145732
  569.9 55.8 %all-gather.5.cloned.1.call-start = ((), (), s32[]{:S(2)}) async-start(), calls=%async_computation.9 | async-start | bytes 1327104 | tf_op jit(solution)/shard_map/all_gather | solution.py:50
  599.3 117.0 %all-reduce.10.cloned.1.call-start = ((), (), s32[]{:S(2)}) async-start(), calls=%async_computation.10 | async-start | bytes 2097152 | tf_op jit(solution)/shard_map/psum | solution.py:130
  628.3 322.3 %all-reduce.12.cloned.1.call-start = ((), (), s32[]{:S(2)}) async-start(), calls=%async_computation.11 | async-start | bytes 4718592 | tf_op jit(solution)/shard_map/psum | solution.py:55
  716.3 1.7 copy-start.7
  803.3 47.2 %copy-start.5 = (f32[576,512]{1,0:T(8,128)S(1)}, f32[576,512]{1,0:T(8,128)}, u32[]{:S(2)}) copy-start(f32[576,512]{1,0:T(8,128)} %all-gather.5.cloned.1.call-done) | copy-start | bytes 3538948
  811.2 39.3 %copy-start.8 = (f32[512,512]{1,0:T(8,128)}, f32[512,512]{1,0:T(8,128)S(1)}, u32[]{:S(2)}) copy-start(f32[512,512]{1,0:T(8,128)S(1)} %get-tuple-element.216) | copy-start | bytes 3145732
  856.7 2.1 copy-start.10
  856.7 93.9 %copy-start.1 = (f32[576,1152]{1,0:T(8,128)S(1)}, f32[576,1152]{1,0:T(8,128)}, u32[]{:S(2)}) copy-start(f32[576,1152]{1,0:T(8,128)} %copy-done) | copy-start | bytes 7962628
  950.7 7.0 copy-start.12
  970.4 6.7 copy-start.6
  970.4 23.4 %all-to-all-start.2 = ((f32[8,64,576]{2,1,0:T(8,128)}), f32[8,64,576]{2,1,0:T(8,128)S(1)}, u32[]{:S(2)}, u32[]{:S(2)}) async-start(f32[8,64,576]{2,1,0:T(8,128)} %bitcast.63), calls=%async_computation.4 | async-start | bytes 2621440 | tf_op jit(solution)/shard_map/all_to_all | solution.py:60
Sparse Core Ops, SparseCore 0:
  155.6 27.2 reduce-scatter.2
  184.6 24.8 all-gather.2
  213.7 86.8 all-reduce.7
  468.6 91.5 all-reduce.13
  570.0 29.2 reduce-scatter.4
  600.9 24.7 all-gather.4
  629.0 87.3 all-reduce.9
  859.0 91.6 all-reduce.11
where the time goes:
time: 1010 us; the launch traced here: 1000 us
  waiting for transfers between devices  534 us (53%)
  other arithmetic  280 us (28%)
  local copies, waits for them, and re-layouts  87.2 us (9%)
  matrix products  51.5 us (5%)
  starting transfers between devices  28.7 us (3%)
  between operations  20 us (2%)
    psum x2, waiting for transfers between devices, broadcast(): return lax.psum(jnp.where(mine, value, jnp.zeros_like(value)), axis)  183 us
    psum x2, waiting for transfers between devices, per_device(): diag_block = lax.psum(piece, 'row')  174 us
    another operation x29, other arithmetic, per_device(): chol = jnp.linalg.cholesky(0.5 * (diag_block + diag_block.T))  160 us
    another operation x5, other arithmetic, per_device(): solved = jax.scipy.linalg.solve_triangular(chol, panel.T, lower=True).T  81.2 us
    reduce_scatter x2, waiting for transfers between devices, from_root(): own = lax.psum_scatter(padded, axis, scatter_dimension=0, tiled=True)  56.7 us
    all_gather x2, waiting for transfers between devices, from_root(): lax.all_gather(own, axis, axis=0, tiled=True)[:len(lines)]  52.8 us
    all_to_all x2, waiting for transfers between devices, one_exchange(): tiles = lax.all_to_all(tiles, axis, split_axis=0, concat_axis=0, tiled=True)  50.7 us
    all_to_all x2, starting transfers between devices, one_exchange(): tiles = lax.all_to_all(tiles, axis, split_axis=0, concat_axis=0, tiled=True)  20.9 us
  transfers between devices with their start and end apart: 11, of which 10 were waited for; matrix products, arithmetic and copies ran while one was open for 3% of the time, Pallas kernels for 0%

commit v1 on v0

v1 whole, which is shorter than its diff:
```python
import functools

import jax
import jax.numpy as jnp
from jax import lax
from jax.experimental import pallas as pl
from jax.experimental.pallas import tpu as pltpu
from jax.sharding import PartitionSpec as P

NB = 512
PANELS = 2
TB = 64
SLOTS = 32
LANES = 128
SUB = 16
BLK = 128

HIGH = lax.Precision.HIGHEST
GOOD = lax.Precision.HIGH

def factor_rows(rows, base):
    sub = lax.broadcasted_iota(jnp.int32, (8, BLK), 0)
    sub2 = lax.broadcasted_iota(jnp.int32, (8, 2 * BLK), 0)
    spread = [
        [
            jnp.broadcast_to(rows[g][:, base + i : base + i + 1], (8, BLK)) if i < 8 * g + 8 else None
            for i in range(SUB)
        ]
        for g in range(2)
    ]
    rows = list(rows)
    for i in range(SUB):
        own, at = divmod(i, 8)
        pivot = jnp.broadcast_to(spread[own][i][at : at + 1, :], (8, BLK))
        scale = lax.rsqrt(pivot)
        scale2 = jnp.concatenate([scale, scale], axis=1)
        line = jnp.broadcast_to(rows[own][at : at + 1, :], (8, 2 * BLK)) * scale2
        lows = []
        for g in range(2):
            if g < own:
                lows.append(None)
                continue
            low = spread[g][i] * scale
            if g == own:
                low = jnp.where(sub > at, low, 0.0)
            lows.append(low)
        for j in range(i + 1, SUB):
            g_j, at_j = divmod(j, 8)
            factor = jnp.broadcast_to(lows[g_j][at_j : at_j + 1, :], (8, BLK))
            for g in range(g_j, 2):
                spread[g][j] = spread[g][j] - lows[g] * factor
        for g in range(own, 2):
            low2 = jnp.concatenate([lows[g], lows[g]], axis=1)
            new = rows[g] - low2 * line
            if g == own:
                new = jnp.where(sub2 == at, line, new)
            rows[g] = new
    return rows


def inverse_factor(x_ref):
    for s in range(BLK // SUB):
        base = s * SUB
        rows = factor_rows([x_ref[base : base + 8, :], x_ref[base + 8 : base + 16, :]], base)
        x_ref[base : base + 8, :] = rows[0]
        x_ref[base + 8 : base + 16, :] = rows[1]
        if base + SUB < BLK:
            done = jnp.concatenate(rows, axis=0)
            gone = lax.dot_general(
                done[:, :BLK].T, done, (((1,), (0,)), ((), ())), precision=HIGH,
                preferred_element_type=jnp.float32,
            )
            x_ref[base + SUB :, :] = x_ref[base + SUB :, :] - gone[base + SUB :, :]


def cholesky_kernel(d_ref, w_ref, a_ref, x_ref):
    n = d_ref.shape[0]
    blocks = n // BLK
    a_ref[...] = d_ref[...]
    w_ref[...] = jnp.zeros_like(w_ref)
    eye = (
        lax.broadcasted_iota(jnp.int32, (BLK, BLK), 0) == lax.broadcasted_iota(jnp.int32, (BLK, BLK), 1)
    ).astype(jnp.float32)

    def dot(a, b):
        return lax.dot_general(a, b, (((1,), (0,)), ((), ())), precision=HIGH, preferred_element_type=jnp.float32)

    for b in range(blocks):
        lo, hi = b * BLK, (b + 1) * BLK
        diag = a_ref[lo:hi, lo:hi]
        x_ref[:, :BLK] = 0.5 * (diag + diag.T)
        x_ref[:, BLK:] = eye
        inverse_factor(x_ref)
        w_diag = x_ref[:, BLK:]
        w_ref[lo:hi, lo:hi] = w_diag
        if b:
            w_ref[lo:hi, :lo] = dot(w_diag, w_ref[lo:hi, :lo])
        if b + 1 < blocks:
            upper = dot(w_diag, a_ref[lo:hi, hi:])
            a_ref[lo:hi, hi:] = upper
            for i in range(b + 1, blocks):
                low, top = i * BLK, (i + 1) * BLK
                left = a_ref[lo:hi, low:top].T
                a_ref[low:top, low:] = a_ref[low:top, low:] - dot(left, a_ref[lo:hi, low:])
                w_ref[low:top, :hi] = w_ref[low:top, :hi] - dot(left, w_ref[lo:hi, :hi])


def inverse_of_factor(d):
    n = d.shape[0]
    return pl.pallas_call(
        cholesky_kernel,
        out_shape=jax.ShapeDtypeStruct((n, n), jnp.float32),
        in_specs=[pl.BlockSpec(memory_space=pltpu.VMEM)],
        out_specs=pl.BlockSpec(memory_space=pltpu.VMEM),
        scratch_shapes=[pltpu.VMEM((n, n), jnp.float32), pltpu.VMEM((BLK, 2 * BLK), jnp.float32)],
        compiler_params=pltpu.CompilerParams(vmem_limit_bytes=48 << 20),
        cost_estimate=pl.CostEstimate(flops=2_000_000_000, bytes_accessed=8 << 20, transcendentals=0),
        name="inverse_of_factor",
    )(d)


def pack_kernel(source_ref, tiles_ref, out_ref, laid_ref, *, pitch, unroll):
    held = tiles_ref.shape[0]
    chunks = tiles_ref.shape[1] // LANES
    for group in range(held // 8):
        for part in range(chunks):
            laid_ref[pl.ds(group * 8 * pitch + part, 8, stride=pitch), :] = tiles_ref[
                group * 8 : group * 8 + 8, part * LANES : (part + 1) * LANES
            ]

    def step(q, carry):
        start = pl.multiple_of(source_ref[q] * pitch, 8)
        out_ref[q] = laid_ref[pl.ds(start, chunks), :]
        return carry

    lax.fori_loop(0, out_ref.shape[0], step, 0, unroll=unroll)


def packed(tiles, source):
    held, width = tiles.shape
    chunks = width // LANES
    pitch = chunks + 8
    return pl.pallas_call(
        functools.partial(pack_kernel, pitch=pitch, unroll=4),
        out_shape=jax.ShapeDtypeStruct((source.shape[0], chunks, LANES), jnp.float32),
        in_specs=[pl.BlockSpec(memory_space=pltpu.SMEM), pl.BlockSpec(memory_space=pltpu.VMEM)],
        out_specs=pl.BlockSpec(memory_space=pltpu.VMEM),
        scratch_shapes=[pltpu.VMEM((held * pitch, LANES), jnp.float32)],
        compiler_params=pltpu.CompilerParams(vmem_limit_bytes=32 << 20),
        cost_estimate=pl.CostEstimate(flops=10_000_000, bytes_accessed=6 << 20, transcendentals=0),
        name="packed_tiles",
    )(source, tiles)


def place_kernel(code_ref, tiles_ref, front_ref, out_ref, sum_ref, *, unroll):
    rows, cols = front_ref.shape
    blocks = cols // LANES
    flips = -(-rows // LANES)
    half_rows = TB * TB // LANES
    sum_ref[...] = jnp.zeros_like(sum_ref)
    left = lax.broadcasted_iota(jnp.int32, (half_rows, LANES), 1) < TB

    def step(q, carry):
        code = code_ref[q]
        start = pl.multiple_of((code // 2) * TB, TB)
        odd = code % 2
        tile = tiles_ref[q]
        turned = pltpu.roll(tile, TB, 1)
        is_left = odd == 0
        keep = left == is_left
        upper = jnp.where(keep, jnp.where(is_left, tile, turned), 0.0)
        lower = jnp.where(keep, jnp.where(is_left, turned, tile), 0.0)
        even = pl.ds(start, half_rows, stride=2)
        uneven = pl.ds(start + 1, half_rows, stride=2)
        sum_ref[even, :] = sum_ref[even, :] + upper
        sum_ref[uneven, :] = sum_ref[uneven, :] + lower
        return carry

    lax.fori_loop(0, tiles_ref.shape[0], step, 0, unroll=unroll)
    for block in range(blocks):
        lo, hi = block * LANES, (block + 1) * LANES
        out_ref[:, lo:hi] = front_ref[:, lo:hi] + sum_ref[block * rows : (block + 1) * rows, :]
        for flip in range(flips):
            at = blocks * rows + flip * cols + lo
            size = min(LANES, rows - flip * LANES)
            span = slice(flip * LANES, flip * LANES + size)
            out_ref[span, lo:hi] = out_ref[span, lo:hi] + sum_ref[at : at + LANES, :].T[:size, :]


def placed(front, tiles, code):
    rows, cols = front.shape
    total = (cols // LANES) * rows + -(-rows // LANES) * cols + TB
    return pl.pallas_call(
        functools.partial(place_kernel, unroll=8),
        out_shape=jax.ShapeDtypeStruct(front.shape, jnp.float32),
        in_specs=[pl.BlockSpec(memory_space=pltpu.SMEM)] + [pl.BlockSpec(memory_space=pltpu.VMEM)] * 2,
        out_specs=pl.BlockSpec(memory_space=pltpu.VMEM),
        scratch_shapes=[pltpu.VMEM((total, LANES), jnp.float32)],
        compiler_params=pltpu.CompilerParams(vmem_limit_bytes=32 << 20),
        cost_estimate=pl.CostEstimate(flops=10_000_000, bytes_accessed=10 << 20, transcendentals=0),
        name="placed_tiles",
    )(code, tiles, front)


MESH = pl.DeviceIdType.MESH


def share_kernel(
    matrix_ref, z_ref, y_ref, d_ref, z_all_ref, y_own_ref,
    z_in, y_in, first_send, next_send, d_recv, z_send, z_recv, zall_send, zall_recv, y_send, y_recv,
):
    me_row, me_col = lax.axis_index("row"), lax.axis_index("col")
    n_row, n_col = z_in.shape[0], y_in.shape[0]
    order = d_ref.shape[0]
    local_rows = matrix_ref.shape[0]
    piece = order // n_row
    z_lines, y_lines = z_in.shape[1], y_in.shape[1]

    def y_copy(step):
        to = lax.rem(me_col + step, n_col)
        return pltpu.make_async_remote_copy(
            y_ref.at[pl.ds(pl.multiple_of(to * y_lines, 8), y_lines)], y_in.at[me_col],
            y_send.at[to], y_recv.at[me_col], device_id=(me_row, to), device_id_type=MESH,
        )

    def z_copy(step):
        to = lax.rem(me_row + step, n_row)
        return pltpu.make_async_remote_copy(
            z_ref.at[pl.ds(pl.multiple_of(to * z_lines, 8), z_lines)], z_in.at[me_row],
            z_send.at[to], z_recv.at[me_row], device_id=(to, me_col), device_id_type=MESH,
        )

    def z_all_copy(step):
        to = lax.rem(me_row + step, n_row)
        mine = z_all_ref.at[pl.ds(pl.multiple_of(me_row * z_lines, 8), z_lines)]
        return pltpu.make_async_remote_copy(
            mine, mine, zall_send.at[to], zall_recv.at[me_row], device_id=(to, me_col), device_id_type=MESH,
        )

    def cut(j):
        return j * piece // 128 * 128

    def d_piece(j):
        return d_ref.at[j * piece : (j + 1) * piece, cut(j) : order]

    def arrived(into, sem):
        pltpu.make_async_copy(into, into, sem).wait()

    def first_copy(j):
        at = j * piece % local_rows
        return pltpu.make_async_remote_copy(
            matrix_ref.at[at : at + piece, cut(j) : order],
            d_piece(j),
            first_send.at[j], d_recv.at[j], device_id=(j, me_col), device_id_type=MESH,
        )

    def next_copy(j, step):
        to = lax.rem(j + step, n_row)
        here = d_piece(j)
        source = matrix_ref.at[0:piece, 0:order] if j == 0 else here
        return pltpu.make_async_remote_copy(
            source, here, next_send.at[to], d_recv.at[j], device_id=(to, me_col), device_id_type=MESH,
        )

    def each(count, action):
        def step(s, carry):
            action(s)
            return carry
        lax.fori_loop(1, count, step, 0)

    for root in range(2):
        @pl.when((me_col == 0) & (me_row == root))
        def _():
            for j in range(max(1, root * local_rows // piece), min(n_row, (root + 1) * local_rows // piece)):
                first_copy(j).start()
            if root == 0:
                d_ref[0:piece, :] = matrix_ref[0:piece, 0:order]
                each(n_row, lambda s: next_copy(0, s).start())

    @pl.when(me_col == 0)
    def _():
        each(n_row, lambda s: z_copy(s).start())

    each(n_col, lambda s: y_copy(s).start())

    for j in range(1, n_row):
        @pl.when((me_col == 0) & (me_row == j))
        def _():
            arrived(d_piece(j), d_recv.at[j])
            each(n_row, lambda s: next_copy(j, s).start())

    @pl.when(me_col == 0)
    def _():
        own = pl.ds(pl.multiple_of(me_row * z_lines, 8), z_lines)
        z_in[me_row] = z_ref[own, :]
        each(n_row, lambda s: arrived(z_in.at[lax.rem(me_row + s, n_row)], z_recv.at[lax.rem(me_row + s, n_row)]))
        total = z_in[0]
        for k in range(1, n_row):
            total = total + z_in[k]
        z_all_ref[own, :] = total

    each(n_col, lambda s: arrived(y_in.at[lax.rem(me_col + s, n_col)], y_recv.at[lax.rem(me_col + s, n_col)]))
    y_in[me_col] = y_ref[pl.ds(pl.multiple_of(me_col * y_lines, 8), y_lines), :]
    y_total = y_in[0]
    for k in range(1, n_col):
        y_total = y_total + y_in[k]
    y_own_ref[...] = y_total

    @pl.when(me_col == 0)
    def _():
        each(n_row, lambda s: z_all_copy(s).start())
        for j in range(n_row):
            @pl.when(me_row != j)
            def _():
                arrived(d_piece(j), d_recv.at[j])
                arrived(z_all_ref.at[j * z_lines : (j + 1) * z_lines], zall_recv.at[j])

        each(n_row, lambda s: z_copy(s).wait_send())
        each(n_row, lambda s: z_all_copy(s).wait_send())

    each(n_col, lambda s: y_copy(s).wait_send())
    for root in range(2):
        @pl.when((me_col == 0) & (me_row == root))
        def _():
            for j in range(max(1, root * local_rows // piece), min(n_row, (root + 1) * local_rows // piece)):
                first_copy(j).wait_send()
    for j in range(n_row):
        @pl.when((me_col == 0) & (me_row == j))
        def _():
            each(n_row, lambda s: next_copy(j, s).wait_send())


def shared(matrix, z_part, y_part, order, n_row, n_col):
    lines_z, lines_y = z_part.shape[0] // n_row, y_part.shape[0] // n_col
    dma = pltpu.SemaphoreType.DMA
    return pl.pallas_call(
        share_kernel,
        out_shape=(
            jax.ShapeDtypeStruct((order, order), jnp.float32),
            jax.ShapeDtypeStruct(z_part.shape, jnp.float32),
            jax.ShapeDtypeStruct((lines_y, y_part.shape[1]), jnp.float32),
        ),
        in_specs=[pl.BlockSpec(memory_space=pltpu.VMEM)] * 3,
        out_specs=[pl.BlockSpec(memory_space=pltpu.VMEM)] * 3,
        scratch_shapes=[
            pltpu.VMEM((n_row, lines_z, z_part.shape[1]), jnp.float32),
            pltpu.VMEM((n_col, lines_y, y_part.shape[1]), jnp.float32),
            *[dma((n_row,))] * 7,
            *[dma((n_col,))] * 2,
        ],
        compiler_params=pltpu.CompilerParams(has_side_effects=True, vmem_limit_bytes=40 << 20),
        cost_estimate=pl.CostEstimate(flops=1_000_000_000, bytes_accessed=12 << 20, transcendentals=0),
        name="shared_parts",
    )(matrix, z_part, y_part)


def hand_out_kernel(solved_ref, fix_ref, panel_ref, share_ref, solved_send, solved_recv, fix_send, fix_recv):
    me_row, me_col = lax.axis_index("row"), lax.axis_index("col")
    n_col = solved_ref.shape[0]
    lines = share_ref.shape[0]

    def copies(to):
        return (
            pltpu.make_async_remote_copy(
                solved_ref.at[to], panel_ref, solved_send.at[to], solved_recv.at[0],
                device_id=(me_row, to), device_id_type=MESH,
            ),
            pltpu.make_async_remote_copy(
                fix_ref.at[pl.ds(pl.multiple_of(to * lines, 8), lines)], share_ref,
                fix_send.at[to], fix_recv.at[0], device_id=(me_row, to), device_id_type=MESH,
            ),
        )

    def each(action):
        def step(to, carry):
            action(to)
            return carry
        lax.fori_loop(1, n_col, step, 0)

    def begin(to):
        for copy in copies(to):
            copy.start()

    def finish(to):
        for copy in copies(to):
            copy.wait_send()

    @pl.when(me_col == 0)
    def _():
        each(begin)
        panel_ref[...] = solved_ref[0]
        share_ref[...] = fix_ref[0:lines, :]
        each(finish)

    @pl.when(me_col != 0)
    def _():
        pltpu.make_async_copy(panel_ref, panel_ref, solved_recv.at[0]).wait()
        pltpu.make_async_copy(share_ref, share_ref, fix_recv.at[0]).wait()


def handed_out(solved, fix):
    n_col, rows, width = solved.shape
    dma = pltpu.SemaphoreType.DMA
    return pl.pallas_call(
        hand_out_kernel,
        out_shape=(
            jax.ShapeDtypeStruct((rows, width), jnp.float32),
            jax.ShapeDtypeStruct((fix.shape[0] // n_col, fix.shape[1]), jnp.float32),
        ),
        in_specs=[pl.BlockSpec(memory_space=pltpu.VMEM)] * 2,
        out_specs=[pl.BlockSpec(memory_space=pltpu.VMEM)] * 2,
        scratch_shapes=[dma((n_col,)), dma((1,)), dma((n_col,)), dma((1,))],
        compiler_params=pltpu.CompilerParams(has_side_effects=True, vmem_limit_bytes=24 << 20),
        cost_estimate=pl.CostEstimate(flops=1_000_000_000, bytes_accessed=8 << 20, transcendentals=0),
        name="handed_out",
    )(solved, fix)


def per_device(front, child_tiles, tile_target, tile_count, probe):
    n_row, n_col = lax.axis_size("row"), lax.axis_size("col")
    devices = n_row * n_col
    me_row, me_col = lax.axis_index("row"), lax.axis_index("col")
    rows, cols = front.shape
    tile_rows, tile_cols = rows // TB, cols // TB
    grid = tile_cols * n_col
    held = child_tiles.shape[0]
    start = PANELS * NB
    slot_index = jnp.arange(held, dtype=jnp.int32)
    live = slot_index % SLOTS < tile_count[slot_index // SLOTS]
    first_row, first_col = tile_target // grid, tile_target % grid
    target_row = jnp.concatenate([first_row, first_col])
    target_col = jnp.concatenate([first_col, first_row])
    owner = target_row // tile_rows * n_col + target_col // tile_cols
    in_row, in_col = target_row % tile_rows, target_col % tile_cols
    upright = jnp.arange(2 * held) < held
    upright_code = 2 * (in_col // 2 * tile_rows + in_row) + in_col % 2
    blocks = cols // LANES * tile_rows
    flips = -(-rows // LANES) * tile_cols
    turned_code = 2 * (blocks + in_row // 2 * tile_cols + in_col) + in_row % 2
    code = jnp.where(upright, upright_code, turned_code)
    code = jnp.where(jnp.concatenate([live, live]), code, 2 * (blocks + flips))
    order = jnp.arange(2 * held, dtype=jnp.int32)
    same = (owner[:, None] == owner[None, :]) & (order[None, :] < order[:, None])
    slot = 2 * owner + jnp.sum(same.astype(jnp.int32), axis=1)
    at_slot = slot[None, :] == order[:, None]
    source = jnp.sum(jnp.where(at_slot, (order % held)[None, :], 0), axis=1)
    sent_code = jnp.sum(jnp.where(at_slot, code[None, :], 0), axis=1)
    outgoing = packed(child_tiles, source)
    chunks = outgoing.shape[1]
    incoming = lax.all_to_all(
        outgoing.reshape(devices, 2, chunks, LANES), ("row", "col"), split_axis=0, concat_axis=0, tiled=True
    )
    landing = lax.all_to_all(
        sent_code.reshape(devices, 2), ("row", "col"), split_axis=0, concat_axis=0, tiled=True
    )
    group = n_row // n_col
    half = lax.dynamic_slice_in_dim(probe, me_row % group * rows, rows, 0)
    probe_rows = lax.ppermute(
        half, ("row", "col"), [(r * n_col + r // group, r * n_col) for r in range(n_row)]
    )
    matrix = placed(front, incoming.reshape(2 * devices, chunks, LANES), landing.reshape(-1))

    global_rows = me_row * rows + jnp.arange(rows, dtype=jnp.int32)
    global_cols = me_col * cols + jnp.arange(cols, dtype=jnp.int32)
    by_cols = jnp.where((global_cols >= start)[:, None], probe, 0.0)
    by_rows = jnp.where((global_rows >= start)[:, None], probe_rows, 0.0)
    y_part = lax.dot_general(by_cols, matrix, (((0,), (1,)), ((), ())), precision=GOOD)
    panel = matrix[:, :start]
    z_part = lax.dot_general(by_rows, panel, (((0,), (0,)), ((), ())), precision=GOOD)
    leading, z_all, y_own = shared(matrix, z_part, y_part, start, n_row, n_col)
    inverse = inverse_of_factor(leading)
    solved = lax.dot_general(panel, inverse, (((1,), (1,)), ((), ())), precision=GOOD)
    panel_of = jnp.arange(start, dtype=jnp.int32) // NB * NB
    solved = jnp.where(global_rows[:, None] >= panel_of[None, :], solved, 0.0)
    weights = lax.dot_general(z_all, inverse, (((1,), (1,)), ((), ())), precision=GOOD)
    fix = lax.dot_general(weights, solved, (((1,), (1,)), ((), ())), precision=GOOD)
    by_owner = solved.reshape(rows, n_col, start // n_col).transpose(1, 0, 2)
    panel_factor, fix_own = handed_out(by_owner, fix)
    sketch = jnp.where((global_rows >= start)[:, None], (y_own - fix_own).T, 0.0)
    return (panel_factor, sketch)


def solution(mesh):
    return jax.shard_map(
        per_device,
        mesh=mesh,
        in_specs=(
            P("row", "col"),
            P(("row", "col"), None),
            P(("row", "col")),
            P(("row", "col")),
            P("col", None),
        ),
        out_specs=(P("row", "col"), P("row", "col")),
        check_vma=False,
    )
```

time: 1010 us -> 286 us (0.28)
  the two profiles are of different devices: /device:TPU:9 before, /device:TPU:17 now
where the time goes in v1:
time: 286 us; the launch traced here: 282 us
  Pallas kernels  178 us (62%)
  waiting for transfers between devices  46.3 us (16%)
  starting transfers between devices  20.4 us (7%)
  matrix products  20.4 us (7%)
  local copies, waits for them, and re-layouts  11.5 us (4%)
  other arithmetic  5.29 us (2%)
    pallas_call x1, Pallas kernels, handed_out(): pl.pallas_call(hand_out_kernel, out_shape=(jax.ShapeDtypeStruct((rows, wi...  80.4 us
    pallas_call x1, Pallas kernels, inverse_of_factor(): pl.pallas_call(cholesky_kernel, out_shape=jax.ShapeDtypeStruct((n, n), jn...  52.6 us
    all_to_all x1, waiting for transfers between devices, per_device(): lax.all_to_all(outgoing.reshape(devices, 2, chunks, LANES), ('row', 'col'...  43.7 us
    pallas_call x1, Pallas kernels, shared(): pl.pallas_call(share_kernel, out_shape=(jax.ShapeDtypeStruct((order, orde...  36 us
    all_to_all x1, starting transfers between devices, per_device(): lax.all_to_all(sent_code.reshape(devices, 2), ('row', 'col'), split_axis=...  10.6 us
    all_to_all x1, starting transfers between devices, per_device(): lax.all_to_all(outgoing.reshape(devices, 2, chunks, LANES), ('row', 'col'...  7.6 us
    pallas_call x1, Pallas kernels, placed(): pl.pallas_call(functools.partial(place_kernel, unroll=8), out_shape=jax.S...  7.16 us
    unnamed x11, local copies, waits for them, and re-layouts  6.19 us
  transfers between devices with their start and end apart: 3, of which 2 were waited for; matrix products, arithmetic and copies ran while one was open for 3% of the time, Pallas kernels for 3%

profile of v1, /device:TPU:17, one launch (start us, length us, event | category | flops | bytes accessed | tf_op | source)
XLA Modules:
  0.0 282.4 jit_solution(14966394706357643318)
XLA Ops:
  0.6 1.4 fusion.29
  2.0 0.7 and_select_fusion.11
  2.7 2.5 fusion.24
  5.2 0.2 convert_reduce_fusion
  5.4 0.2 select_reduce_fusion
  5.6 0.8 all_to_all.9
  6.4 10.6 %all-to-all-start = ((s32[128,1,2]{2,1,0:T(1,128)}), s32[128,1,2]{2,1,0:T(1,128)S(1)}, u32[]{:S(2)}, u32[]{:S(2)}) async-start(s32[128,1,2]{2,1,0:T(1,128)} %bitcast.5), calls=%async_computation | async-start | bytes 131072 | tf_op jit(solution)/shard_map/all_to_all | solution.py:453
  17.0 0.0 copy-start.3
  17.0 1.6 copy-done.3
  18.6 1.5 packed_tiles.1
  20.1 0.0 copy-start
  20.1 2.0 copy-done
  22.1 2.6 all-to-all-done
  24.7 0.0 copy-start.2
  24.7 7.6 %all-to-all-start.1 = ((f32[128,2,32,128]{3,2,1,0:T(8,128)}), f32[128,2,32,128]{3,2,1,0:T(8,128)}, u32[]{:S(2)}, u32[]{:S(2)}) async-start(f32[128,2,32,128]{3,2,1,0:T(8,128)} %bitcast.25), calls=%async_computation.1 | async-start | bytes 8388608 | tf_op jit(solution)/shard_map/all_to_all | solution.py:450
  32.3 2.5 constant_dynamic-slice_fusion
  34.8 2.2 collective-permute-start
  37.0 0.5 broadcast.488
  37.5 0.8 reduce.3
  38.4 0.1 reshape.434.code_ref
  38.5 43.7 %all-to-all-done.1 = f32[128,2,32,128]{3,2,1,0:T(8,128)} async-done(((f32[128,2,32,128]{3,2,1,0:T(8,128)}), f32[128,2,32,128]{3,2,1,0:T(8,128)}, u32[]{:S(2)}, u32[]{:S(2)}) %all-to-all-start.1) | async-done | bytes 4194336 | tf_op jit(solution)/shard_map/all_to_all | solution.py:450
  82.2 0.0 copy-done.2
  82.2 0.0 copy-start.4
  82.2 7.2 %placed_tiles.1.matrix_ref = f32[576,1152]{1,0:T(8,128)S(1)} custom-call(s32[256]{0:T(256)S(1)} %reshape.434.code_ref, f32[256,32,128]{2,1,0:T(8,128)} %bitcast.7.tiles_ref, f32[576,1152]{1,0:T(8,128)S(1)} %copy-done.2), custom_call_target="tpu_custom_call" | custom-call | flops 10000000 | bytes 10485760 | tf_op jit(solution)/shard_map/placed_tiles/pallas_call | solution.py:193
  89.3 0.0 copy-done.4
  89.3 5.9 %fusion.y_ref = f32[512,576]{1,0:T(8,128)S(1)} fusion(f32[576,1152]{1,0:T(8,128)S(1)} %placed_tiles.1.matrix_ref, f32[1152,512]{1,0:T(8,128)S(1)} %copy-done.4, pred[1152]{0:T(1024)(128)(4,1)S(1)} %add_compare_fusion), kind=kOutput, calls=%fused_computation.1 | convolution fusion | flops 2039021568 | bytes 6194304 | tf_op jit(solution)/shard_map/dot_general | solution.py:467
  95.2 0.0 collective-permute-done
  95.2 4.0 %fusion.4.z_ref = f32[512,1024]{1,0:T(8,128)S(1)} fusion(f32[576,1152]{1,0:T(8,128)S(1)} %placed_tiles.1.matrix_ref, f32[576,512]{1,0:T(8,128)} %collective-permute-done, pred[576]{0:T(1024)(128)(4,1)S(1)} %broadcast_compare_fusion), kind=kOutput, calls=%fused_computation.6 | convolution fusion | flops 1812234240 | bytes 5637120 | tf_op jit(solution)/shard_map/dot_general | solution.py:469
  99.2 36.0 %shared_parts.1 = (f32[1024,1024]{1,0:T(8,128)S(1)}, f32[512,1024]{1,0:T(8,128)S(1)}, f32[64,576]{1,0:T(8,128)S(1)}) custom-call(f32[576,1152]{1,0:T(8,128)S(1)} %placed_tiles.1.matrix_ref, f32[512,1024]{1,0:T(8,128)S(1)} %fusion.4.z_ref, f32[512,576]{1,0:T(8,128)S(1)} %fusion.y_ref), custom_call_target="tpu_custom_call" | custom-call | flops 1000000000 | bytes 12582912 | tf_op jit(solution)/shard_map/shared_parts/pallas_call | solution.py:336
  135.2 0.0 copy-start.1
  135.2 1.9 copy-done.1
  137.2 52.6 %inverse_of_factor.1 = f32[1024,1024]{1,0:T(8,128)S(1)} custom-call(f32[1024,1024]{1,0:T(8,128)} %copy-done.1), custom_call_target="tpu_custom_call" | custom-call | flops 2000000000 | bytes 8388608 | tf_op jit(solution)/shard_map/inverse_of_factor/pallas_call | solution.py:110
  189.7 4.1 %fusion.2 = f32[576,1024]{1,0:T(8,128)S(1)} fusion(f32[1024,1024]{1,0:T(8,128)S(1)} %inverse_of_factor.1, f32[576,1152]{1,0:T(8,128)S(1)} %placed_tiles.1.matrix_ref), kind=kOutput, calls=%fused_computation.4 | convolution fusion | flops 3623878656 | bytes 8912896 | tf_op jit(solution)/shard_map/dot_general | solution.py:472
  193.9 3.5 %fusion.30 = f32[512,1024]{1,0:T(8,128)S(1)} fusion(f32[512,1024]{1,0:T(8,128)S(1)} %get-tuple-element.8, f32[1024,1024]{1,0:T(8,128)S(1)} %inverse_of_factor.1), kind=kOutput, calls=%fused_computation.79 | convolution fusion | flops 3221225472 | bytes 8388608 | tf_op jit(solution)/shard_map/dot_general | solution.py:475
  197.4 0.2 bitcast_bitcast_fusion.solved_ref
  197.6 2.8 %fusion.6.fix_ref = f32[512,576]{1,0:T(8,128)S(1)} fusion(f32[512,1024]{1,0:T(8,128)S(1)} %fusion.30, f32[576,1024]{1,0:T(8,128)S(1)} %fusion.2, s32[1024]{0:T(1024)S(1)} %fusion.17, s32[576]{0:T(1024)S(1)} %iota_add_fusion), kind=kOutput, calls=%fused_computation.8 | convolution fusion | flops 1813118976 | bytes 5642496 | tf_op jit(solution)/shard_map/dot_general | solution.py:476
  200.5 80.4 %handed_out.1 = (f32[576,128]{1,0:T(8,128)S(1)}, f32[64,576]{1,0:T(8,128)S(1)}) custom-call(f32[8,576,128]{2,1,0:T(8,128)S(1)} %bitcast_bitcast_fusion.solved_ref, f32[512,576]{1,0:T(8,128)S(1)} %fusion.6.fix_ref), custom_call_target="tpu_custom_call" | custom-call | flops 1000000000 | bytes 8388608 | tf_op jit(solution)/shard_map/handed_out/pallas_call | solution.py:404
  280.8 0.7 select_bitcast_fusion
  281.5 0.7 copy.25
  (6 shorter events, 0.1 us)
Async XLA Ops:
  6.4 18.3 %all-to-all-start = ((s32[128,1,2]{2,1,0:T(1,128)}), s32[128,1,2]{2,1,0:T(1,128)S(1)}, u32[]{:S(2)}, u32[]{:S(2)}) async-start(s32[128,1,2]{2,1,0:T(1,128)} %bitcast.5), calls=%async_computation | async-start | bytes 131072 | tf_op jit(solution)/shard_map/all_to_all | solution.py:453
  17.0 1.6 copy-start.3
  20.1 2.0 copy-start
  24.7 57.5 %copy-start.2 = (f32[576,1152]{1,0:T(8,128)S(1)}, f32[576,1152]{1,0:T(8,128)}, u32[]{:S(2)}) copy-start(f32[576,1152]{1,0:T(8,128)} %front_ref.1) | copy-start | bytes 7962628
  24.7 57.5 %all-to-all-start.1 = ((f32[128,2,32,128]{3,2,1,0:T(8,128)}), f32[128,2,32,128]{3,2,1,0:T(8,128)}, u32[]{:S(2)}, u32[]{:S(2)}) async-start(f32[128,2,32,128]{3,2,1,0:T(8,128)} %bitcast.25), calls=%async_computation.1 | async-start | bytes 8388608 | tf_op jit(solution)/shard_map/all_to_all | solution.py:450
  34.8 60.4 %collective-permute-start = (f32[576,512]{1,0:T(8,128)}, f32[576,512]{1,0:T(8,128)}, u32[]{:S(2)}, u32[]{:S(2)}) collective-permute-start(f32[576,512]{1,0:T(8,128)} %constant_dynamic-slice_fusion), channel_id=1, source_target_pairs={{0,0},{8,8},{17,16},{25,24},{34,32},{42,40},{51,48},{59,56},{68,64... | collective-permute-start | bytes 3538952 | tf_op jit(solution)/shard_map/ppermute | solution.py:458
  82.2 7.2 %copy-start.4 = (f32[1152,512]{1,0:T(8,128)S(1)}, f32[1152,512]{1,0:T(8,128)}, u32[]{:S(2)}) copy-start(f32[1152,512]{1,0:T(8,128)} %param.9) | copy-start | bytes 7077892
  135.2 1.9 copy-start.1

commit v2 on v1

v2 whole, which is shorter than its diff:
```python
import functools

import jax
import jax.numpy as jnp
from jax import lax
from jax.experimental import pallas as pl
from jax.experimental.pallas import tpu as pltpu
from jax.sharding import PartitionSpec as P

NB = 512
PANELS = 2
TB = 64
SLOTS = 32
LANES = 128
SUB = 16
BLK = 128

HIGH = lax.Precision.HIGHEST
GOOD = lax.Precision.HIGH


def pack_kernel(source_ref, tiles_ref, out_ref, laid_ref, *, pitch, unroll):
    held = tiles_ref.shape[0]
    chunks = tiles_ref.shape[1] // LANES
    for group in range(held // 8):
        for part in range(chunks):
            laid_ref[pl.ds(group * 8 * pitch + part, 8, stride=pitch), :] = tiles_ref[
                group * 8 : group * 8 + 8, part * LANES : (part + 1) * LANES
            ]

    def step(q, carry):
        start = pl.multiple_of(source_ref[q] * pitch, 8)
        out_ref[q] = laid_ref[pl.ds(start, chunks), :]
        return carry

    lax.fori_loop(0, out_ref.shape[0], step, 0, unroll=unroll)


def packed(tiles, source):
    held, width = tiles.shape
    chunks = width // LANES
    pitch = chunks + 8
    return pl.pallas_call(
        functools.partial(pack_kernel, pitch=pitch, unroll=4),
        out_shape=jax.ShapeDtypeStruct((source.shape[0], chunks, LANES), jnp.float32),
        in_specs=[pl.BlockSpec(memory_space=pltpu.SMEM), pl.BlockSpec(memory_space=pltpu.VMEM)],
        out_specs=pl.BlockSpec(memory_space=pltpu.VMEM),
        scratch_shapes=[pltpu.VMEM((held * pitch, LANES), jnp.float32)],
        compiler_params=pltpu.CompilerParams(vmem_limit_bytes=32 << 20),
        cost_estimate=pl.CostEstimate(flops=10_000_000, bytes_accessed=6 << 20, transcendentals=0),
        name="packed_tiles",
    )(source, tiles)


def place_kernel(code_ref, tiles_ref, front_ref, out_ref, sum_ref, *, unroll):
    rows, cols = front_ref.shape
    blocks = cols // LANES
    flips = -(-rows // LANES)
    half_rows = TB * TB // LANES
    sum_ref[...] = jnp.zeros_like(sum_ref)
    left = lax.broadcasted_iota(jnp.int32, (half_rows, LANES), 1) < TB

    def step(q, carry):
        code = code_ref[q]
        start = pl.multiple_of((code // 2) * TB, TB)
        odd = code % 2
        tile = tiles_ref[q]
        turned = pltpu.roll(tile, TB, 1)
        is_left = odd == 0
        keep = left == is_left
        upper = jnp.where(keep, jnp.where(is_left, tile, turned), 0.0)
        lower = jnp.where(keep, jnp.where(is_left, turned, tile), 0.0)
        even = pl.ds(start, half_rows, stride=2)
        uneven = pl.ds(start + 1, half_rows, stride=2)
        sum_ref[even, :] = sum_ref[even, :] + upper
        sum_ref[uneven, :] = sum_ref[uneven, :] + lower
        return carry

    lax.fori_loop(0, tiles_ref.shape[0], step, 0, unroll=unroll)
    for block in range(blocks):
        lo, hi = block * LANES, (block + 1) * LANES
        out_ref[:, lo:hi] = front_ref[:, lo:hi] + sum_ref[block * rows : (block + 1) * rows, :]
        for flip in range(flips):
            at = blocks * rows + flip * cols + lo
            size = min(LANES, rows - flip * LANES)
            span = slice(flip * LANES, flip * LANES + size)
            out_ref[span, lo:hi] = out_ref[span, lo:hi] + sum_ref[at : at + LANES, :].T[:size, :]


def placed(front, tiles, code):
    rows, cols = front.shape
    total = (cols // LANES) * rows + -(-rows // LANES) * cols + TB
    return pl.pallas_call(
        functools.partial(place_kernel, unroll=8),
        out_shape=jax.ShapeDtypeStruct(front.shape, jnp.float32),
        in_specs=[pl.BlockSpec(memory_space=pltpu.SMEM)] + [pl.BlockSpec(memory_space=pltpu.VMEM)] * 2,
        out_specs=pl.BlockSpec(memory_space=pltpu.VMEM),
        scratch_shapes=[pltpu.VMEM((total, LANES), jnp.float32)],
        compiler_params=pltpu.CompilerParams(vmem_limit_bytes=32 << 20),
        cost_estimate=pl.CostEstimate(flops=10_000_000, bytes_accessed=10 << 20, transcendentals=0),
        name="placed_tiles",
    )(code, tiles, front)


MESH = pl.DeviceIdType.MESH


def exchange_kernel(
    tiles_ref, code_ref, probe_ref, tiles_in, code_in, probe_rows,
    tiles_send, tiles_recv, code_send, code_recv, probe_send, probe_recv,
):
    n_row, n_col = lax.axis_size("row"), lax.axis_size("col")
    devices = n_row * n_col
    me_row, me_col = lax.axis_index("row"), lax.axis_index("col")
    me = me_row * n_col + me_col
    rows = probe_rows.shape[0]
    group = n_row // n_col
    at = pl.ds(pl.multiple_of(lax.rem(me_row, group) * rows, 8), rows)

    def copies(step):
        to = lax.rem(me + step, devices)
        where_to = (to // n_col, lax.rem(to, n_col))
        return (
            pltpu.make_async_remote_copy(
                code_ref.at[to], code_in.at[me], code_send, code_recv,
                device_id=where_to, device_id_type=MESH,
            ),
            pltpu.make_async_remote_copy(
                tiles_ref.at[to], tiles_in.at[me], tiles_send, tiles_recv,
                device_id=where_to, device_id_type=MESH,
            ),
        )

    def begin(step, carry):
        for copy in copies(step):
            copy.start()
        return carry

    probe_copy = pltpu.make_async_remote_copy(
        probe_ref.at[at], probe_rows, probe_send, probe_recv, device_id=(me_row, 0), device_id_type=MESH
    )
    source_col = me_row // group
    sends_probe = (me_col == source_col) & (me_col != 0)
    gets_probe = (me_col == 0) & (source_col != 0)

    lax.fori_loop(1, devices, begin, 0)

    @pl.when(sends_probe)
    def _():
        probe_copy.start()

    @pl.when((me_col == 0) & (source_col == 0))
    def _():
        probe_rows[...] = probe_ref[at, :]

    tiles_in[me] = tiles_ref[me]
    code_in[me] = code_ref[me]
    others = pl.ds(0, devices - 1)

    def all_of(ref, sem):
        pltpu.make_async_copy(ref.at[others], ref.at[others], sem).wait()

    all_of(code_in, code_recv)
    all_of(tiles_in, tiles_recv)
    all_of(code_ref, code_send)
    all_of(tiles_ref, tiles_send)

    @pl.when(gets_probe)
    def _():
        pltpu.make_async_copy(probe_rows, probe_rows, probe_recv).wait()

    @pl.when(sends_probe)
    def _():
        probe_copy.wait_send()


def exchanged(tiles, code, probe, rows):
    dma = pltpu.SemaphoreType.DMA
    return pl.pallas_call(
        exchange_kernel,
        out_shape=(
            jax.ShapeDtypeStruct(tiles.shape, jnp.float32),
            jax.ShapeDtypeStruct(code.shape, jnp.int32),
            jax.ShapeDtypeStruct((rows, probe.shape[1]), jnp.float32),
        ),
        in_specs=[pl.BlockSpec(memory_space=pltpu.VMEM)] * 3,
        out_specs=[pl.BlockSpec(memory_space=pltpu.VMEM)] * 3,
        scratch_shapes=[dma] * 6,
        compiler_params=pltpu.CompilerParams(has_side_effects=True, vmem_limit_bytes=32 << 20),
        cost_estimate=pl.CostEstimate(flops=1_000_000_000, bytes_accessed=16 << 20, transcendentals=0),
        name="exchanged_tiles",
    )(tiles, code, probe)


def factor_rows(rows, base):
    sub = lax.broadcasted_iota(jnp.int32, (8, BLK), 0)
    lane = lax.broadcasted_iota(jnp.int32, (8, BLK), 1)

    def column(g, i):
        here = jnp.where(lane == base + i, rows[g][:, :BLK], 0.0)
        return jnp.broadcast_to(jnp.sum(here, axis=1, keepdims=True), (8, BLK))

    spread = [[column(g, i) if i < 8 * g + 8 else None for i in range(SUB)] for g in range(2)]
    halves = [[row[:, :BLK], row[:, BLK:]] for row in rows]
    for i in range(SUB):
        own, at = divmod(i, 8)
        pivot = jnp.broadcast_to(spread[own][i][at : at + 1, :], (8, BLK))
        scale = lax.rsqrt(pivot)
        lows = [None, None]
        for g in range(own, 2):
            low = spread[g][i] * scale
            lows[g] = jnp.where(sub > at, low, 0.0) if g == own else low
        for j in range(i + 1, SUB):
            g_j, at_j = divmod(j, 8)
            factor = jnp.broadcast_to(lows[g_j][at_j : at_j + 1, :], (8, BLK))
            for g in range(g_j, 2):
                spread[g][j] = spread[g][j] - lows[g] * factor
        for h in range(2):
            line = jnp.broadcast_to(halves[own][h][at : at + 1, :], (8, BLK)) * scale
            for g in range(own, 2):
                new = halves[g][h] - lows[g] * line
                halves[g][h] = jnp.where(sub == at, line, new) if g == own else new
    return [jnp.concatenate(half, axis=1) for half in halves]


def inverse_factor(x_ref, beside):
    row = lax.broadcasted_iota(jnp.int32, (BLK, 2 * BLK), 0)

    def step(s, carry):
        base = pl.multiple_of(s * SUB, SUB)
        rows = factor_rows([x_ref[pl.ds(base, 8), :], x_ref[pl.ds(base + 8, 8), :]], base)
        beside(s)
        x_ref[pl.ds(base, 8), :] = rows[0]
        x_ref[pl.ds(base + 8, 8), :] = rows[1]
        done = jnp.concatenate(rows, axis=0)
        gone = plain_dot(done[:, :BLK].T, done)
        x_ref[...] = x_ref[...] - jnp.where(row >= base + SUB, gone, 0.0)
        return carry

    lax.fori_loop(0, BLK // SUB, step, 0)


def plain_dot(a, b):
    return lax.dot_general(
        a, b, (((1,), (0,)), ((), ())), precision=HIGH, preferred_element_type=jnp.float32
    )


def halves_of(a):
    top = a.astype(jnp.bfloat16)
    return top, (a - top.astype(jnp.float32)).astype(jnp.bfloat16)


def turned_dot(a, b):
    a_top, a_rest = halves_of(a)
    b_top, b_rest = halves_of(b)

    def part(p, q):
        return lax.dot_general(p, q, (((1,), (1,)), ((), ())), preferred_element_type=jnp.float32)

    return part(a_top, b_top) + (part(a_top, b_rest) + part(a_rest, b_top))


def panel_kernel(
    matrix_ref, z_ref, y_ref, w_ref, solved_ref, panel_ref, z_all_ref, y_own_ref,
    m_ref, stage_ref, x_ref, z_in, y_in,
    first_send, first_recv, next_send, d_recv, z_send, z_recv, zall_send, zall_recv,
    y_send, y_recv, s_send, s_recv,
):
    me_row, me_col = lax.axis_index("row"), lax.axis_index("col")
    n_row, n_col = z_in.shape[0], y_in.shape[0]
    blocks, _, order = m_ref.shape
    rows = matrix_ref.shape[0]
    piece = order // n_row
    per_block = BLK // piece
    z_lines, y_lines = z_in.shape[1], y_in.shape[1]
    on_panel = me_col == 0

    def y_copy(step):
        to = lax.rem(me_col + step, n_col)
        return pltpu.make_async_remote_copy(
            y_ref.at[pl.ds(pl.multiple_of(to * y_lines, 8), y_lines)], y_in.at[me_col],
            y_send.at[to], y_recv.at[me_col], device_id=(me_row, to), device_id_type=MESH,
        )

    def z_copy(step):
        to = lax.rem(me_row + step, n_row)
        return pltpu.make_async_remote_copy(
            z_ref.at[pl.ds(pl.multiple_of(to * z_lines, 8), z_lines)], z_in.at[me_row],
            z_send.at[to], z_recv.at[me_row], device_id=(to, me_col), device_id_type=MESH,
        )

    def z_all_copy(step):
        to = lax.rem(me_row + step, n_row)
        mine = z_all_ref.at[pl.ds(pl.multiple_of(me_row * z_lines, 8), z_lines)]
        return pltpu.make_async_remote_copy(
            mine, mine, zall_send.at[to], zall_recv.at[me_row], device_id=(to, me_col), device_id_type=MESH,
        )

    def solved_copy(i):
        return pltpu.make_async_remote_copy(
            solved_ref.at[i], panel_ref, s_send.at[i], s_recv.at[0],
            device_id=(me_row, i), device_id_type=MESH,
        )

    def cut(j):
        return j // per_block * BLK

    def d_piece(j):
        at = j % per_block * piece
        return m_ref.at[j // per_block, at : at + piece, cut(j) : order]

    def from_root(j):
        at = j * piece % rows
        return matrix_ref.at[at : at + piece, cut(j) : order]

    def arrived(into, sem):
        pltpu.make_async_copy(into, into, sem).wait()

    def first_copy(j):
        return pltpu.make_async_remote_copy(
            from_root(j), stage_ref.at[:, cut(j) : order],
            first_send.at[j], first_recv.at[0], device_id=(j, me_col), device_id_type=MESH,
        )

    def next_copy(j, step):
        to = lax.rem(j + step, n_row)
        source = stage_ref.at[:, cut(j) : order] if j else from_root(0)
        return pltpu.make_async_remote_copy(
            source, d_piece(j), next_send.at[to], d_recv.at[j], device_id=(to, me_col), device_id_type=MESH,
        )

    def each(count, action):
        def step(s, carry):
            action(s)
            return carry

        lax.fori_loop(1, count, step, 0)

    roots = [
        [j for j in range(1, n_row) if j * piece // rows == root] for root in range(-(-order // rows))
    ]
    for root, pieces in enumerate(roots):
        @pl.when(on_panel & (me_row == root))
        def _(pieces=pieces):
            for j in pieces:
                first_copy(j).start()

    for j in range(n_row):
        @pl.when(on_panel & (me_row == j))
        def _(j=j):
            at = j % per_block * piece
            if j:
                arrived(stage_ref.at[:, cut(j) : order], first_recv.at[0])
                each(n_row, lambda s: next_copy(j, s).start())
                m_ref[j // per_block, at : at + piece, cut(j) : order] = stage_ref[:, cut(j) : order]
            else:
                each(n_row, lambda s: next_copy(j, s).start())
                m_ref[0, 0:piece, :] = matrix_ref[0:piece, 0:order]

    @pl.when(on_panel)
    def _():
        each(n_row, lambda s: z_copy(s).start())

    each(n_col, lambda s: y_copy(s).start())

    def sum_z():
        own = pl.ds(pl.multiple_of(me_row * z_lines, 8), z_lines)
        z_in[me_row] = z_ref[own, :]

        def wait_z(s):
            k = lax.rem(me_row + s, n_row)
            arrived(z_in.at[k], z_recv.at[k])

        each(n_row, wait_z)
        total = z_in[0]
        for k in range(1, n_row):
            total = total + z_in[k]
        z_all_ref[own, :] = total

    def sum_y():
        def wait_y(s):
            k = lax.rem(me_col + s, n_col)
            arrived(y_in.at[k], y_recv.at[k])

        each(n_col, wait_y)
        y_in[me_col] = y_ref[pl.ds(pl.multiple_of(me_col * y_lines, 8), y_lines), :]
        y_total = y_in[0]
        for k in range(1, n_col):
            y_total = y_total + y_in[k]
        y_own_ref[...] = y_total

    eye = (
        lax.broadcasted_iota(jnp.int32, (BLK, BLK), 0) == lax.broadcasted_iota(jnp.int32, (BLK, BLK), 1)
    ).astype(jnp.float32)
    slab = rows // (BLK // SUB)

    def solve_slab(i, s):
        lines = pl.ds(pl.multiple_of(s * slab, 8), slab)
        hi = (i + 1) * BLK
        part = turned_dot(matrix_ref[lines, :hi], w_ref[i, :, :hi])
        if i * BLK >= NB:
            line = me_row * rows + s * slab + lax.broadcasted_iota(jnp.int32, (slab, BLK), 0)
            part = jnp.where(line >= i * BLK // NB * NB, part, 0.0)
        solved_ref[i, lines, :] = part

    @pl.when(on_panel)
    def _():
        for i in range(blocks):
            lo, hi = i * BLK, (i + 1) * BLK
            for j in range(i * per_block, (i + 1) * per_block):
                @pl.when(me_row != j)
                def _(j=j):
                    arrived(d_piece(j), d_recv.at[j])
            own_row = m_ref[i, :, lo:]
            if i:
                left = jnp.concatenate([m_ref[b, :, lo:hi].T for b in range(i)], axis=1)
                own_row = own_row - plain_dot(left, m_ref[:i, :, lo:].reshape(lo, order - lo))
                w_ref[i, :, :lo] = -plain_dot(left, w_ref[:i, :, :lo].reshape(lo, lo))
            diag = own_row[:, :BLK]
            x_ref[:, :BLK] = 0.5 * (diag + diag.T)
            x_ref[:, BLK:] = eye
            if hi < order:
                m_ref[i, :, hi:] = own_row[:, BLK:]
            inverse_factor(x_ref, (lambda s: solve_slab(i - 1, s)) if i else (lambda s: None))
            if i > 1:
                solved_copy(i - 1).start()
            if i == 3:
                sum_z()
            w_diag = x_ref[:, BLK:]
            w_ref[i, :, lo:hi] = w_diag
            if i:
                w_ref[i, :, :lo] = plain_dot(w_diag, w_ref[i, :, :lo])
            if hi < order:
                m_ref[i, :, hi:] = plain_dot(w_diag, m_ref[i, :, hi:])
                w_ref[i, :, hi:] = jnp.zeros((BLK, order - hi), jnp.float32)
            if i == 4:
                each(n_row, lambda s: z_all_copy(s).start())

        def last(s, carry):
            solve_slab(blocks - 1, s)
            return carry

        lax.fori_loop(0, BLK // SUB, last, 0)

    sum_y()

    @pl.when(on_panel)
    def _():
        solved_copy(blocks - 1).start()
        panel_ref[...] = solved_ref[0]

        def wait_all(s):
            k = lax.rem(me_row + s, n_row)
            lines = z_all_ref.at[pl.ds(pl.multiple_of(k * z_lines, 8), z_lines)]
            arrived(lines, zall_recv.at[k])

        each(n_row, wait_all)
        each(n_row, lambda s: z_copy(s).wait_send())
        each(n_row, lambda s: z_all_copy(s).wait_send())
        each(n_col, lambda s: solved_copy(s).wait_send())

    @pl.when(me_col != 0)
    def _():
        arrived(panel_ref, s_recv.at[0])

    each(n_col, lambda s: y_copy(s).wait_send())
    for root, pieces in enumerate(roots):
        @pl.when(on_panel & (me_row == root))
        def _(pieces=pieces):
            for j in pieces:
                first_copy(j).wait_send()
    for j in range(n_row):
        @pl.when(on_panel & (me_row == j))
        def _(j=j):
            each(n_row, lambda s: next_copy(j, s).wait_send())


def panel_parts(matrix, z_part, y_part, order, n_row, n_col):
    lines_z, lines_y = z_part.shape[0] // n_row, y_part.shape[0] // n_col
    rows = matrix.shape[0]
    width = order // n_col
    dma = pltpu.SemaphoreType.DMA
    whole = functools.partial(jax.ShapeDtypeStruct, dtype=jnp.float32)
    return pl.pallas_call(
        panel_kernel,
        out_shape=(
            whole((order // BLK, BLK, order)),
            whole((n_col, rows, width)),
            whole((rows, width)),
            whole(z_part.shape),
            whole((lines_y, y_part.shape[1])),
        ),
        in_specs=[pl.BlockSpec(memory_space=pltpu.VMEM)] * 3,
        out_specs=[pl.BlockSpec(memory_space=pltpu.VMEM)] * 5,
        scratch_shapes=[
            pltpu.VMEM((order // BLK, BLK, order), jnp.float32),
            pltpu.VMEM((order // n_row, order), jnp.float32),
            pltpu.VMEM((BLK, 2 * BLK), jnp.float32),
            pltpu.VMEM((n_row, lines_z, z_part.shape[1]), jnp.float32),
            pltpu.VMEM((n_col, lines_y, y_part.shape[1]), jnp.float32),
            dma((n_row,)), dma((1,)), *[dma((n_row,))] * 6, *[dma((n_col,))] * 2, dma((n_col,)), dma((1,)),
        ],
        compiler_params=pltpu.CompilerParams(has_side_effects=True, vmem_limit_bytes=60 << 20),
        cost_estimate=pl.CostEstimate(flops=3_000_000_000, bytes_accessed=16 << 20, transcendentals=0),
        name="panel_parts",
    )(matrix, z_part, y_part)


def hand_out_kernel(fix_ref, share_ref, fix_send, fix_recv):
    me_row, me_col = lax.axis_index("row"), lax.axis_index("col")
    lines = share_ref.shape[0]
    n_col = fix_ref.shape[0] // lines

    def copy(to):
        return pltpu.make_async_remote_copy(
            fix_ref.at[pl.ds(pl.multiple_of(to * lines, 8), lines)], share_ref,
            fix_send.at[to], fix_recv.at[0], device_id=(me_row, to), device_id_type=MESH,
        )

    @pl.when(me_col == 0)
    def _():
        for to in range(1, n_col):
            copy(to).start()
        share_ref[...] = fix_ref[0:lines, :]
        for to in range(1, n_col):
            copy(to).wait_send()

    @pl.when(me_col != 0)
    def _():
        pltpu.make_async_copy(share_ref, share_ref, fix_recv.at[0]).wait()


def handed_out(fix, n_col):
    dma = pltpu.SemaphoreType.DMA
    return pl.pallas_call(
        hand_out_kernel,
        out_shape=jax.ShapeDtypeStruct((fix.shape[0] // n_col, fix.shape[1]), jnp.float32),
        in_specs=[pl.BlockSpec(memory_space=pltpu.VMEM)],
        out_specs=pl.BlockSpec(memory_space=pltpu.VMEM),
        scratch_shapes=[dma((n_col,)), dma((1,))],
        compiler_params=pltpu.CompilerParams(has_side_effects=True, vmem_limit_bytes=16 << 20),
        cost_estimate=pl.CostEstimate(flops=1_000_000_000, bytes_accessed=4 << 20, transcendentals=0),
        name="handed_out",
    )(fix)


def per_device(front, child_tiles, tile_target, tile_count, probe):
    n_row, n_col = lax.axis_size("row"), lax.axis_size("col")
    devices = n_row * n_col
    me_row, me_col = lax.axis_index("row"), lax.axis_index("col")
    rows, cols = front.shape
    tile_rows, tile_cols = rows // TB, cols // TB
    grid = tile_cols * n_col
    held = child_tiles.shape[0]
    start = PANELS * NB
    slot_index = jnp.arange(held, dtype=jnp.int32)
    live = slot_index % SLOTS < tile_count[slot_index // SLOTS]
    first_row, first_col = tile_target // grid, tile_target % grid
    target_row = jnp.concatenate([first_row, first_col])
    target_col = jnp.concatenate([first_col, first_row])
    owner = target_row // tile_rows * n_col + target_col // tile_cols
    in_row, in_col = target_row % tile_rows, target_col % tile_cols
    upright = jnp.arange(2 * held) < held
    upright_code = 2 * (in_col // 2 * tile_rows + in_row) + in_col % 2
    blocks = cols // LANES * tile_rows
    flips = -(-rows // LANES) * tile_cols
    turned_code = 2 * (blocks + in_row // 2 * tile_cols + in_col) + in_row % 2
    code = jnp.where(upright, upright_code, turned_code)
    code = jnp.where(jnp.concatenate([live, live]), code, 2 * (blocks + flips))
    order = jnp.arange(2 * held, dtype=jnp.int32)
    same = (owner[:, None] == owner[None, :]) & (order[None, :] < order[:, None])
    slot = 2 * owner + jnp.sum(same.astype(jnp.int32), axis=1)
    at_slot = slot[None, :] == order[:, None]
    source = jnp.sum(jnp.where(at_slot, (order % held)[None, :], 0), axis=1)
    sent_code = jnp.sum(jnp.where(at_slot, code[None, :], 0), axis=1)
    outgoing = packed(child_tiles, source)
    chunks = outgoing.shape[1]
    code_lines = jnp.pad(sent_code.reshape(devices, 1, 2), ((0, 0), (0, 0), (0, LANES - 2)))
    incoming, landing, probe_rows = exchanged(
        outgoing.reshape(devices, 2 * chunks, LANES), code_lines, probe, rows
    )
    matrix = placed(front, incoming.reshape(2 * devices, chunks, LANES), landing[:, 0, :2].reshape(-1))

    global_rows = me_row * rows + jnp.arange(rows, dtype=jnp.int32)
    global_cols = me_col * cols + jnp.arange(cols, dtype=jnp.int32)
    by_cols = jnp.where((global_cols >= start)[:, None], probe, 0.0)
    by_rows = jnp.where((global_rows >= start)[:, None], probe_rows, 0.0)
    y_part = lax.dot_general(by_cols, matrix, (((0,), (1,)), ((), ())), precision=GOOD)
    panel = matrix[:, :start]
    z_part = lax.dot_general(by_rows, panel, (((0,), (0,)), ((), ())), precision=GOOD)
    inverse, solved, panel_factor, z_all, y_own = panel_parts(matrix, z_part, y_part, start, n_row, n_col)
    weights = lax.dot_general(
        z_all, inverse.reshape(start, start), (((1,), (1,)), ((), ())), precision=GOOD
    )
    fix = lax.dot_general(
        weights.reshape(-1, n_col, start // n_col), solved, (((1, 2), (0, 2)), ((), ())), precision=GOOD
    )
    fix_own = handed_out(fix, n_col)
    sketch = jnp.where((global_rows >= start)[:, None], (y_own - fix_own).T, 0.0)
    return (panel_factor, sketch)


def solution(mesh):
    return jax.shard_map(
        per_device,
        mesh=mesh,
        in_specs=(
            P("row", "col"),
            P(("row", "col"), None),
            P(("row", "col")),
            P(("row", "col")),
            P("col", None),
        ),
        out_specs=(P("row", "col"), P("row", "col")),
        check_vma=False,
    )
```

time: 286 us -> 272 us (0.951)
  the two profiles are of different devices: /device:TPU:17 before, /device:TPU:9 now
where the time goes in v2:
time: 272 us; the launch traced here: 268 us
  Pallas kernels  232 us (85%)
  matrix products  20.1 us (7%)
  local copies, waits for them, and re-layouts  10.3 us (4%)
  other arithmetic  4.31 us (2%)
    pallas_call x1, Pallas kernels, panel_parts(): pl.pallas_call(panel_kernel, out_shape=(whole((order // BLK, BLK, order))...  83.3 us
    pallas_call x1, Pallas kernels, exchanged(): pl.pallas_call(exchange_kernel, out_shape=(jax.ShapeDtypeStruct(tiles.sha...  77.1 us
    pallas_call x1, Pallas kernels, handed_out(): pl.pallas_call(hand_out_kernel, out_shape=jax.ShapeDtypeStruct((fix.shape...  65.1 us
    unnamed x21, local copies, waits for them, and re-layouts  8.32 us
    dot_general x1, matrix products, per_device(): lax.dot_general(by_cols, matrix, (((0,), (1,)), ((), ())), precision=GOOD)  6.96 us
    dot_general x1, matrix products, per_device(): lax.dot_general(z_all, inverse.reshape(start, start), (((1,), (1,)), ((),...  6.23 us

profile of v2, /device:TPU:9, one launch (start us, length us, event | category | flops | bytes accessed | tf_op | source)
XLA Modules:
  0.0 267.9 jit_solution(17350407998769638437)
XLA Ops:
  0.6 0.7 and_select_fusion.11
  1.3 1.5 fusion.19
  2.8 2.6 fusion.15
  5.4 0.2 convert_reduce_fusion
  5.6 0.2 select_reduce_fusion
  5.8 0.1 reshape.415
  6.0 0.0 copy-start.6
  6.0 1.6 copy-done.6
  7.6 0.0 copy-start.1
  7.6 1.5 packed_tiles.1
  9.1 0.1 copy-done.1
  9.2 77.1 %exchanged_tiles.1 = (f32[128,64,128]{2,1,0:T(8,128)S(1)}, s32[128,1,128]{2,1,0:T(1,128)S(1)}, f32[576,512]{1,0:T(8,128)S(1)}) custom-call(f32[128,64,128]{2,1,0:T(8,128)S(1)} %bitcast.22, s32[128,1,128]{2,1,0:T(1,128)S(1)} %pad.4.code_ref, f32[1152,512]{1,0:T(8,128)S(1)} %copy-done.1), custom_call_target="tpu_custom_call" | custom-call | flops 1000000000 | bytes 16777216 | tf_op jit(solution)/shard_map/exchanged_tiles/pallas_call | solution.py:179
  86.3 0.0 copy-start.3
  86.4 1.9 copy-done.3
  88.3 0.2 slice_reduce_fusion
  88.5 0.1 reshape_squeeze.3.code_ref
  88.6 0.0 copy-start.4
  88.6 2.2 copy-done.4
  90.8 0.0 copy-start.5
  90.8 1.7 copy-done.5
  92.5 5.4 %placed_tiles.1.matrix_ref = f32[576,1152]{1,0:T(8,128)S(1)} custom-call(s32[256]{0:T(256)S(1)} %reshape_squeeze.3.code_ref, f32[256,32,128]{2,1,0:T(8,128)S(1)} %bitcast.23, f32[576,1152]{1,0:T(8,128)S(1)} %copy-done.5), custom_call_target="tpu_custom_call" | custom-call | flops 10000000 | bytes 10485760 | tf_op jit(solution)/shard_map/placed_tiles/pallas_call | solution.py:93
  97.9 0.0 copy-start
  97.9 0.0 copy-start.2
  97.9 4.1 %fusion.z_ref = f32[512,1024]{1,0:T(8,128)} fusion(f32[576,1152]{1,0:T(8,128)S(1)} %placed_tiles.1.matrix_ref, f32[576,512]{1,0:T(8,128)S(1)} %get-tuple-element.12, pred[576]{0:T(1024)(128)(4,1)S(1)} %add_compare_fusion.1), kind=kOutput, calls=%fused_computation | convolution fusion | flops 1812234240 | bytes 5637120 | tf_op jit(solution)/shard_map/dot_general | solution.py:591
  102.0 0.0 copy-done
  102.0 0.0 copy-done.2
  102.0 7.0 %fusion.2.y_ref = f32[512,576]{1,0:T(8,128)} fusion(f32[576,1152]{1,0:T(8,128)S(1)} %placed_tiles.1.matrix_ref, f32[1152,512]{1,0:T(8,128)S(1)} %copy-done.2, pred[1152]{0:T(1024)(128)(4,1)S(1)} %add_compare_fusion), kind=kOutput, calls=%fused_computation.2 | convolution fusion | flops 2039021568 | bytes 6194304 | tf_op jit(solution)/shard_map/dot_general | solution.py:589
  109.0 83.3 %panel_parts.1 = (f32[8,128,1024]{2,1,0:T(8,128)}, f32[8,576,128]{2,1,0:T(8,128)}, f32[576,128]{1,0:T(8,128)}, f32[512,1024]{1,0:T(8,128)}, f32[64,576]{1,0:T(8,128)}) custom-call(f32[576,1152]{1,0:T(8,128)} %copy-done, f32[512,1024]{1,0:T(8,128)} %fusion.z_ref, f32[512,576]{1,0:T(8,128)} %fusion.2.y_ref), custom_call_target="tpu_custom_call" | custom-call | flops 3000000000 | bytes 16777216 | tf_op jit(solution)/shard_map/panel_parts/pallas_call | solution.py:485
  192.3 0.0 copy-start.7
  192.3 6.2 %fusion.4 = f32[512,8,128]{2,0,1:T(8,128)S(1)} fusion(f32[8,128,1024]{2,1,0:T(8,128)} %get-tuple-element.16, f32[512,1024]{1,0:T(8,128)} %get-tuple-element.15), kind=kOutput, calls=%fused_computation.4 | convolution fusion | flops 3221225472 | bytes 8388608 | tf_op jit(solution)/shard_map/dot_general | solution.py:593
  198.5 0.0 copy-done.7
  198.5 2.8 %convolution_bitcast_fusion.fix_ref = f32[512,576]{1,0:T(8,128)S(1)} fusion(f32[512,8,128]{2,0,1:T(8,128)S(1)} %fusion.4, f32[8,576,128]{2,1,0:T(8,128)S(1)} %copy-done.7), kind=kOutput, calls=%fused_computation.6 | convolution fusion | flops 1811939328 | bytes 5636096 | tf_op jit(solution)/shard_map/dot_general | solution.py:596
  201.3 0.0 copy-start.9
  201.3 0.0 copy-start.8
  201.3 65.1 %handed_out.1 = f32[64,576]{1,0:T(8,128)S(1)} custom-call(f32[512,576]{1,0:T(8,128)S(1)} %convolution_bitcast_fusion.fix_ref), custom_call_target="tpu_custom_call" | custom-call | flops 1000000000 | bytes 4194304 | tf_op jit(solution)/shard_map/handed_out/pallas_call | solution.py:536
  266.5 0.0 copy-done.9
  266.5 0.7 select_bitcast_fusion
  267.1 0.0 copy-done.8
  267.2 0.7 copy.19
  (5 shorter events, 0.1 us)
Async XLA Ops:
  6.0 1.6 copy-start.6
  7.6 1.7 copy-start.1
  86.3 1.9 copy-start.3
  88.6 2.2 copy-start.4
  90.8 1.7 copy-start.5
  97.9 4.1 %copy-start = (f32[576,1152]{1,0:T(8,128)}, f32[576,1152]{1,0:T(8,128)S(1)}, u32[]{:S(2)}) copy-start(f32[576,1152]{1,0:T(8,128)S(1)} %placed_tiles.1.matrix_ref) | copy-start | bytes 7962628
  97.9 4.1 %copy-start.2 = (f32[1152,512]{1,0:T(8,128)S(1)}, f32[1152,512]{1,0:T(8,128)}, u32[]{:S(2)}) copy-start(f32[1152,512]{1,0:T(8,128)} %probe_ref.1) | copy-start | bytes 7077892
  192.3 6.3 %copy-start.7 = (f32[8,576,128]{2,1,0:T(8,128)S(1)}, f32[8,576,128]{2,1,0:T(8,128)}, u32[]{:S(2)}) copy-start(f32[8,576,128]{2,1,0:T(8,128)} %get-tuple-element.17) | copy-start | bytes 7077892
  201.3 65.1 %copy-start.9 = (f32[64,576]{1,0:T(8,128)S(1)}, f32[64,576]{1,0:T(8,128)}, u32[]{:S(2)}) copy-start(f32[64,576]{1,0:T(8,128)} %get-tuple-element.14) | copy-start | bytes 442372
  201.3 65.8 %copy-start.8 = (f32[576,128]{1,0:T(8,128)S(1)}, f32[576,128]{1,0:T(8,128)}, u32[]{:S(2)}) copy-start(f32[576,128]{1,0:T(8,128)} %get-tuple-element.32) | copy-start | bytes 884740

commit v3 on v2

--- a/solution.py
+++ b/solution.py
@@ -118,8 +118,12 @@
     at = pl.ds(pl.multiple_of(lax.rem(me_row, group) * rows, 8), rows)
 
     def copies(step):
-        to = lax.rem(me + step, devices)
-        where_to = (to // n_col, lax.rem(to, n_col))
+        turn = lax.rem(step * 53, devices)
+        across = lax.rem(me_row // 4 + turn // 32, n_row // 4)
+        deep = lax.rem(me_row + turn // 8, 4)
+        up = lax.rem(me_col // 2 + lax.rem(turn // 2, n_col // 2), n_col // 2)
+        where_to = (across * 4 + deep, up * 2 + lax.rem(me_col + turn, 2))
+        to = where_to[0] * n_col + where_to[1]
         return (
             pltpu.make_async_remote_copy(
                 code_ref.at[to], code_in.at[me], code_send, code_recv,
@@ -262,19 +266,24 @@
 
 
 def panel_kernel(
-    matrix_ref, z_ref, y_ref, w_ref, solved_ref, panel_ref, z_all_ref, y_own_ref,
-    m_ref, stage_ref, x_ref, z_in, y_in,
+    matrix_ref, z_ref, y_ref, panel_ref, y_own_ref, share_ref,
+    w_ref, solved_ref, z_all_ref, fix_ref, m_ref, stage_ref, x_ref, z_in, y_in,
     first_send, first_recv, next_send, d_recv, z_send, z_recv, zall_send, zall_recv,
-    y_send, y_recv, s_send, s_recv,
+    y_send, y_recv, s_send, s_recv, fix_send, fix_recv,
 ):
     me_row, me_col = lax.axis_index("row"), lax.axis_index("col")
     n_row, n_col = z_in.shape[0], y_in.shape[0]
     blocks, _, order = m_ref.shape
     rows = matrix_ref.shape[0]
-    piece = order // n_row
-    per_block = BLK // piece
+    piece = BLK // n_row
     z_lines, y_lines = z_in.shape[1], y_in.shape[1]
     on_panel = me_col == 0
+
+    def partner(step):
+        turn = lax.rem(step * 7, n_row)
+        side = 4
+        across = lax.rem(me_row // side + turn // side, n_row // side)
+        return across * side + lax.rem(lax.rem(me_row, side) + lax.rem(turn, side), side)
 
     def y_copy(step):
         to = lax.rem(me_col + step, n_col)
@@ -284,14 +293,14 @@
         )
 
     def z_copy(step):
-        to = lax.rem(me_row + step, n_row)
+        to = partner(step)
         return pltpu.make_async_remote_copy(
             z_ref.at[pl.ds(pl.multiple_of(to * z_lines, 8), z_lines)], z_in.at[me_row],
             z_send.at[to], z_recv.at[me_row], device_id=(to, me_col), device_id_type=MESH,
         )
 
     def z_all_copy(step):
-        to = lax.rem(me_row + step, n_row)
+        to = partner(step)
         mine = z_all_ref.at[pl.ds(pl.multiple_of(me_row * z_lines, 8), z_lines)]
         return pltpu.make_async_remote_copy(
             mine, mine, zall_send.at[to], zall_recv.at[me_row], device_id=(to, me_col), device_id_type=MESH,
@@ -303,32 +312,40 @@
             device_id=(me_row, i), device_id_type=MESH,
         )
 
-    def cut(j):
-        return j // per_block * BLK
-
-    def d_piece(j):
-        at = j % per_block * piece
-        return m_ref.at[j // per_block, at : at + piece, cut(j) : order]
-
-    def from_root(j):
-        at = j * piece % rows
-        return matrix_ref.at[at : at + piece, cut(j) : order]
+    def fix_copy(to):
+        return pltpu.make_async_remote_copy(
+            fix_ref.at[to * y_lines : (to + 1) * y_lines], share_ref, fix_send.at[to], fix_recv.at[0],
+            device_id=(me_row, to), device_id_type=MESH,
+        )
 
     def arrived(into, sem):
         pltpu.make_async_copy(into, into, sem).wait()
 
-    def first_copy(j):
+    def first_copy(b, to, root):
+        at = b * BLK + to * piece - root * rows
         return pltpu.make_async_remote_copy(
-            from_root(j), stage_ref.at[:, cut(j) : order],
-            first_send.at[j], first_recv.at[0], device_id=(j, me_col), device_id_type=MESH,
-        )
-
-    def next_copy(j, step):
-        to = lax.rem(j + step, n_row)
-        source = stage_ref.at[:, cut(j) : order] if j else from_root(0)
+            matrix_ref.at[pl.ds(pl.multiple_of(at, 8), piece), b * BLK : order],
+            stage_ref.at[b, :, b * BLK : order],
+            first_send.at[b], first_recv.at[b], device_id=(to, me_col), device_id_type=MESH,
+        )
+
+    own_lines = pl.ds(pl.multiple_of(me_row * piece, 8), piece)
+
+    def held_piece(b, root=None):
+        if root is None:
+            return stage_ref.at[b, :, b * BLK : order]
+        at = b * BLK + root * piece - root * rows
+        return matrix_ref.at[at : at + piece, b * BLK : order]
+
+    def next_copy(b, step, root=None):
+        to = partner(step)
         return pltpu.make_async_remote_copy(
-            source, d_piece(j), next_send.at[to], d_recv.at[j], device_id=(to, me_col), device_id_type=MESH,
-        )
+            held_piece(b, root), m_ref.at[b, own_lines, b * BLK : order], next_send.at[b], d_recv.at[b],
+            device_id=(to, me_col), device_id_type=MESH,
+        )
+
+    def pieces_of(b, count):
+        return m_ref.at[b, 0 : count * piece, b * BLK : order]
 
     def each(count, action):
         def step(s, carry):
@@ -337,30 +354,41 @@
 
         lax.fori_loop(1, count, step, 0)
 
-    roots = [
-        [j for j in range(1, n_row) if j * piece // rows == root] for root in range(-(-order // rows))
-    ]
-    for root, pieces in enumerate(roots):
+    n_roots = -(-order // rows)
+    sent = [[] for _ in range(n_roots)]
+    for root in range(n_roots):
+        for b in range(blocks):
+            first = max(0, root * rows - b * BLK) // piece
+            last = min(BLK, (root + 1) * rows - b * BLK) // piece
+            if first < last:
+                sent[root].append((b, first, last))
+
+    for root in range(n_roots):
         @pl.when(on_panel & (me_row == root))
-        def _(pieces=pieces):
-            for j in pieces:
-                first_copy(j).start()
-
-    for j in range(n_row):
-        @pl.when(on_panel & (me_row == j))
-        def _(j=j):
-            at = j % per_block * piece
-            if j:
-                arrived(stage_ref.at[:, cut(j) : order], first_recv.at[0])
-                each(n_row, lambda s: next_copy(j, s).start())
-                m_ref[j // per_block, at : at + piece, cut(j) : order] = stage_ref[:, cut(j) : order]
-            else:
-                each(n_row, lambda s: next_copy(j, s).start())
-                m_ref[0, 0:piece, :] = matrix_ref[0:piece, 0:order]
-
-    @pl.when(on_panel)
-    def _():
-        each(n_row, lambda s: z_copy(s).start())
+        def _(root=root):
+            for b, first, last in sent[root]:
+                for to in range(first, last):
+                    if to != root:
+                        first_copy(b, to, root).start()
+
+    local = [[b for b, first, last in sent[root] if first <= root < last] for root in range(n_roots)]
+    for b in range(blocks):
+        mine = None
+        for root in range(n_roots):
+            if b in local[root]:
+                mine = root
+
+        @pl.when(on_panel & (me_row != mine))
+        def _(b=b):
+            arrived(held_piece(b), first_recv.at[b])
+            each(n_row, lambda s: next_copy(b, s).start())
+            m_ref[b, own_lines, b * BLK : order] = stage_ref[b, :, b * BLK : order]
+
+        @pl.when(on_panel & (me_row == mine))
+        def _(b=b, mine=mine):
+            each(n_row, lambda s: next_copy(b, s, mine).start())
+            at = b * BLK + mine * piece - mine * rows
+            m_ref[b, own_lines, b * BLK : order] = matrix_ref[at : at + piece, b * BLK : order]
 
     each(n_col, lambda s: y_copy(s).start())
 
@@ -408,10 +436,9 @@
     def _():
         for i in range(blocks):
             lo, hi = i * BLK, (i + 1) * BLK
-            for j in range(i * per_block, (i + 1) * per_block):
-                @pl.when(me_row != j)
-                def _(j=j):
-                    arrived(d_piece(j), d_recv.at[j])
+            arrived(pieces_of(i, n_row - 1), d_recv.at[i])
+            if i == 1:
+                each(n_row, lambda s: z_copy(s).start())
             own_row = m_ref[i, :, lo:]
             if i:
                 left = jnp.concatenate([m_ref[b, :, lo:hi].T for b in range(i)], axis=1)
@@ -425,7 +452,7 @@
             inverse_factor(x_ref, (lambda s: solve_slab(i - 1, s)) if i else (lambda s: None))
             if i > 1:
                 solved_copy(i - 1).start()
-            if i == 3:
+            if i == 4:
                 sum_z()
             w_diag = x_ref[:, BLK:]
             w_ref[i, :, lo:hi] = w_diag
@@ -456,24 +483,40 @@
             arrived(lines, zall_recv.at[k])
 
         each(n_row, wait_all)
+        inverse = w_ref[...].reshape(order, order)
+        weights = turned_dot(z_all_ref[...], inverse)
+        half = fix_ref.shape[0] // 2
+        for part in (1, 0):
+            lines = slice(part * half, (part + 1) * half)
+            total = None
+            for i in range(blocks):
+                term = turned_dot(weights[lines, i * BLK : (i + 1) * BLK], solved_ref[i])
+                total = term if total is None else total + term
+            fix_ref[lines, :] = total
+            for to in range(part * n_col // 2, (part + 1) * n_col // 2):
+                if to:
+                    fix_copy(to).start()
+        share_ref[...] = fix_ref[0:y_lines, :]
         each(n_row, lambda s: z_copy(s).wait_send())
         each(n_row, lambda s: z_all_copy(s).wait_send())
         each(n_col, lambda s: solved_copy(s).wait_send())
+        for to in range(1, n_col):
+            fix_copy(to).wait_send()
+        for b in range(blocks):
+            arrived(pieces_of(b, n_row - 1), next_send.at[b])
 
     @pl.when(me_col != 0)
     def _():
         arrived(panel_ref, s_recv.at[0])
+        arrived(share_ref, fix_recv.at[0])
 
     each(n_col, lambda s: y_copy(s).wait_send())
-    for root, pieces in enumerate(roots):
+    for root in range(n_roots):
         @pl.when(on_panel & (me_row == root))
-        def _(pieces=pieces):
-            for j in pieces:
-                first_copy(j).wait_send()
-    for j in range(n_row):
-        @pl.when(on_panel & (me_row == j))
-        def _(j=j):
-            each(n_row, lambda s: next_copy(j, s).wait_send())
+        def _(root=root):
+            for b, first, last in sent[root]:
+                count = last - first - (first <= root < last)
+                arrived(pieces_of(b, count), first_send.at[b])
 
 
 def panel_parts(matrix, z_part, y_part, order, n_row, n_col):
@@ -485,64 +528,30 @@
     return pl.pallas_call(
         panel_kernel,
         out_shape=(
-            whole((order // BLK, BLK, order)),
-            whole((n_col, rows, width)),
             whole((rows, width)),
-            whole(z_part.shape),
+            whole((lines_y, y_part.shape[1])),
             whole((lines_y, y_part.shape[1])),
         ),
         in_specs=[pl.BlockSpec(memory_space=pltpu.VMEM)] * 3,
-        out_specs=[pl.BlockSpec(memory_space=pltpu.VMEM)] * 5,
+        out_specs=[pl.BlockSpec(memory_space=pltpu.VMEM)] * 3,
         scratch_shapes=[
             pltpu.VMEM((order // BLK, BLK, order), jnp.float32),
-            pltpu.VMEM((order // n_row, order), jnp.float32),
+            pltpu.VMEM((n_col, rows, width), jnp.float32),
+            pltpu.VMEM(z_part.shape, jnp.float32),
+            pltpu.VMEM(y_part.shape, jnp.float32),
+            pltpu.VMEM((order // BLK, BLK, order), jnp.float32),
+            pltpu.VMEM((order // BLK, BLK // n_row, order), jnp.float32),
             pltpu.VMEM((BLK, 2 * BLK), jnp.float32),
             pltpu.VMEM((n_row, lines_z, z_part.shape[1]), jnp.float32),
             pltpu.VMEM((n_col, lines_y, y_part.shape[1]), jnp.float32),
-            dma((n_row,)), dma((1,)), *[dma((n_row,))] * 6, *[dma((n_col,))] * 2, dma((n_col,)), dma((1,)),
+            *[dma((order // BLK,))] * 4,
+            *[dma((n_row,))] * 4,
+            *[dma((n_col,))] * 3, dma((1,)), dma((n_col,)), dma((1,)),
         ],
         compiler_params=pltpu.CompilerParams(has_side_effects=True, vmem_limit_bytes=60 << 20),
         cost_estimate=pl.CostEstimate(flops=3_000_000_000, bytes_accessed=16 << 20, transcendentals=0),
         name="panel_parts",
     )(matrix, z_part, y_part)
-
-
-def hand_out_kernel(fix_ref, share_ref, fix_send, fix_recv):
-    me_row, me_col = lax.axis_index("row"), lax.axis_index("col")
-    lines = share_ref.shape[0]
-    n_col = fix_ref.shape[0] // lines
-
-    def copy(to):
-        return pltpu.make_async_remote_copy(
-            fix_ref.at[pl.ds(pl.multiple_of(to * lines, 8), lines)], share_ref,
-            fix_send.at[to], fix_recv.at[0], device_id=(me_row, to), device_id_type=MESH,
-        )
-
-    @pl.when(me_col == 0)
-    def _():
-        for to in range(1, n_col):
-            copy(to).start()
-        share_ref[...] = fix_ref[0:lines, :]
-        for to in range(1, n_col):
-            copy(to).wait_send()
-
-    @pl.when(me_col != 0)
-    def _():
-        pltpu.make_async_copy(share_ref, share_ref, fix_recv.at[0]).wait()
-
-
-def handed_out(fix, n_col):
-    dma = pltpu.SemaphoreType.DMA
-    return pl.pallas_call(
-        hand_out_kernel,
-        out_shape=jax.ShapeDtypeStruct((fix.shape[0] // n_col, fix.shape[1]), jnp.float32),
-        in_specs=[pl.BlockSpec(memory_space=pltpu.VMEM)],
-        out_specs=pl.BlockSpec(memory_space=pltpu.VMEM),
-        scratch_shapes=[dma((n_col,)), dma((1,))],
-        compiler_params=pltpu.CompilerParams(has_side_effects=True, vmem_limit_bytes=16 << 20),
-        cost_estimate=pl.CostEstimate(flops=1_000_000_000, bytes_accessed=4 << 20, transcendentals=0),
-        name="handed_out",
-    )(fix)
 
 
 def per_device(front, child_tiles, tile_target, tile_count, probe):
@@ -589,14 +598,7 @@
     y_part = lax.dot_general(by_cols, matrix, (((0,), (1,)), ((), ())), precision=GOOD)
     panel = matrix[:, :start]
     z_part = lax.dot_general(by_rows, panel, (((0,), (0,)), ((), ())), precision=GOOD)
-    inverse, solved, panel_factor, z_all, y_own = panel_parts(matrix, z_part, y_part, start, n_row, n_col)
-    weights = lax.dot_general(
-        z_all, inverse.reshape(start, start), (((1,), (1,)), ((), ())), precision=GOOD
-    )
-    fix = lax.dot_general(
-        weights.reshape(-1, n_col, start // n_col), solved, (((1, 2), (0, 2)), ((), ())), precision=GOOD
-    )
-    fix_own = handed_out(fix, n_col)
+    panel_factor, y_own, fix_own = panel_parts(matrix, z_part, y_part, start, n_row, n_col)
     sketch = jnp.where((global_rows >= start)[:, None], (y_own - fix_own).T, 0.0)
     return (panel_factor, sketch)
 

time: 272 us -> 223 us (0.82); the launches traced: 268 us -> 222 us
  Pallas kernels: 232 us -> 185 us
  local copies, waits for them, and re-layouts: 10.3 us -> 16.2 us
  matrix products: 20.1 us -> 14.9 us
    pallas_call x2 -> x1, Pallas kernels: 148 us -> 115 us  [panel_parts(): pl.pallas_call(panel_kernel, out_shape=(whole((rows, width)), whole((line...]
    pallas_call x1, Pallas kernels: 77.1 us -> 63.6 us  [exchanged(): pl.pallas_call(exchange_kernel, out_shape=(jax.ShapeDtypeStruct(tiles.sha...]
    dot_general x2 -> x0, matrix products: 9.03 us -> none  [the longest x1 6.23 us: per_device(): lax.dot_general(z_all, inverse.reshape(start, start), (((1,), (1,)), ((),...]
    unnamed x21 -> x19, local copies, waits for them, and re-layouts: 8.32 us -> 14.3 us
where the time goes in v3:
time: 223 us; the launch traced here: 222 us
  Pallas kernels  185 us (83%)
  local copies, waits for them, and re-layouts  16.2 us (7%)
  matrix products  14.9 us (7%)
  other arithmetic  5.23 us (2%)
    pallas_call x1, Pallas kernels, panel_parts(): pl.pallas_call(panel_kernel, out_shape=(whole((rows, width)), whole((line...  115 us
    pallas_call x1, Pallas kernels, exchanged(): pl.pallas_call(exchange_kernel, out_shape=(jax.ShapeDtypeStruct(tiles.sha...  63.6 us
    unnamed x19, local copies, waits for them, and re-layouts  14.3 us
    dot_general x1, matrix products, per_device(): lax.dot_general(by_cols, matrix, (((0,), (1,)), ((), ())), precision=GOOD)  8.64 us
    dot_general x1, matrix products, per_device(): lax.dot_general(by_rows, panel, (((0,), (0,)), ((), ())), precision=GOOD)  6.25 us
    pallas_call x1, Pallas kernels, placed(): pl.pallas_call(functools.partial(place_kernel, unroll=8), out_shape=jax.S...  5.36 us

profile of v3, /device:TPU:9, one launch (start us, length us, event | category | flops | bytes accessed | tf_op | source)
XLA Modules:
  0.0 222.2 jit_solution(10918934068810633838)
XLA Ops:
  0.6 1.4 fusion.17
  2.0 2.5 %fusion.13 = pred[128]{0:T(512)(128)(4,1)S(1)} fusion(s32[]{:T(128)} %bitcast.1, s32[]{:T(128)} %bitcast.2, s32[]{:T(128)} %bitcast.4, s32[]{:T(128)} %bitcast.3), kind=kLoop, calls=%fused_computation.55 | loop fusion | flops 3072 | bytes 144 | tf_op jit(solution)/shard_map/lt | solution.py:567
  4.5 0.7 and_select_fusion.11
  5.2 0.2 convert_reduce_fusion
  5.4 0.2 select_reduce_fusion
  5.6 0.0 copy-start.7
  5.6 1.6 copy-done.7
  7.2 0.0 copy-start.3
  7.2 1.5 packed_tiles.1
  8.7 0.0 copy-start.1
  8.7 1.9 copy-done.1
  10.6 0.1 reshape.411
  10.8 0.0 copy-done.3
  10.8 0.0 copy-start.2
  10.9 2.2 copy-done.2
  13.0 63.6 %exchanged_tiles.1 = (f32[128,64,128]{2,1,0:T(8,128)S(1)}, s32[128,1,128]{2,1,0:T(1,128)S(1)}, f32[576,512]{1,0:T(8,128)S(1)}) custom-call(f32[128,64,128]{2,1,0:T(8,128)S(1)} %bitcast.14, s32[128,1,128]{2,1,0:T(1,128)S(1)} %pad.4.code_ref, f32[1152,512]{1,0:T(8,128)S(1)} %copy-done.3), custom_call_target="tpu_custom_call" | custom-call | flops 1000000000 | bytes 16777216 | tf_op jit(solution)/shard_map/exchanged_tiles/pallas_call | solution.py:183
  76.6 0.0 copy-start.4
  76.6 1.9 copy-done.4
  78.6 0.0 copy-start.8
  78.6 1.1 copy-done.8
  79.6 0.2 slice_reduce_fusion
  79.8 0.1 reshape_squeeze.3.code_ref
  80.0 0.0 copy-start.5
  80.0 2.2 copy-done.5
  82.1 0.0 copy-start.6
  82.1 1.7 copy-done.6
  83.9 5.4 %placed_tiles.1.matrix_ref = f32[576,1152]{1,0:T(8,128)S(1)} custom-call(s32[256]{0:T(256)S(1)} %reshape_squeeze.3.code_ref, f32[256,32,128]{2,1,0:T(8,128)S(1)} %bitcast.15, f32[576,1152]{1,0:T(8,128)S(1)} %copy-done.6), custom_call_target="tpu_custom_call" | custom-call | flops 10000000 | bytes 10485760 | tf_op jit(solution)/shard_map/placed_tiles/pallas_call | solution.py:93
  89.3 0.0 copy-start
  89.3 6.2 %fusion.z_ref = f32[512,1024]{1,0:T(8,128)} fusion(f32[576,1152]{1,0:T(8,128)S(1)} %placed_tiles.1.matrix_ref, f32[576,512]{1,0:T(8,128)} %copy-done.8, pred[576]{0:T(1024)(128)(4,1)S(1)} %add_compare_fusion.1), kind=kOutput, calls=%fused_computation | convolution fusion | flops 1812234240 | bytes 5637120 | tf_op jit(solution)/shard_map/dot_general | solution.py:600
  95.5 0.0 copy-done
  95.5 8.6 %fusion.2.y_ref = f32[512,576]{1,0:T(8,128)} fusion(f32[576,1152]{1,0:T(8,128)S(1)} %placed_tiles.1.matrix_ref, f32[1152,512]{1,0:T(8,128)} %probe_ref.1, pred[1152]{0:T(1024)(128)(4,1)S(1)} %add_compare_fusion), kind=kOutput, calls=%fused_computation.2 | convolution fusion | flops 2039021568 | bytes 6194304 | tf_op jit(solution)/shard_map/dot_general | solution.py:598
  104.2 114.7 %panel_parts.1 = (f32[576,128]{1,0:T(8,128)}, f32[64,576]{1,0:T(8,128)}, f32[64,576]{1,0:T(8,128)}) custom-call(f32[576,1152]{1,0:T(8,128)} %copy-done, f32[512,1024]{1,0:T(8,128)} %fusion.z_ref, f32[512,576]{1,0:T(8,128)} %fusion.2.y_ref), custom_call_target="tpu_custom_call" | custom-call | flops 3000000000 | bytes 16777216 | tf_op jit(solution)/shard_map/panel_parts/pallas_call | solution.py:528
  218.9 1.7 select_bitcast_fusion
  220.5 1.7 copy.14
  (5 shorter events, 0.1 us)
Async XLA Ops:
  5.6 1.6 copy-start.7
  7.2 3.7 %copy-start.3 = (f32[1152,512]{1,0:T(8,128)S(1)}, f32[1152,512]{1,0:T(8,128)}, u32[]{:S(2)}) copy-start(f32[1152,512]{1,0:T(8,128)} %probe_ref.1) | copy-start | bytes 7077892
  8.7 1.9 copy-start.1
  10.8 2.2 copy-start.2
  76.6 1.9 copy-start.4
  78.6 1.1 copy-start.8
  80.0 2.2 copy-start.5
  82.1 1.7 copy-start.6
  89.3 6.3 %copy-start = (f32[576,1152]{1,0:T(8,128)}, f32[576,1152]{1,0:T(8,128)S(1)}, u32[]{:S(2)}) copy-start(f32[576,1152]{1,0:T(8,128)S(1)} %placed_tiles.1.matrix_ref) | copy-start | bytes 7962628

commit v4 on v3

--- a/solution.py
+++ b/solution.py
@@ -12,11 +12,9 @@
 TB = 64
 SLOTS = 32
 LANES = 128
-SUB = 16
+SUB = 32
+GROUP = 32
 BLK = 128
-
-HIGH = lax.Precision.HIGHEST
-GOOD = lax.Precision.HIGH
 
 
 def pack_kernel(source_ref, tiles_ref, out_ref, laid_ref, *, pitch, unroll):
@@ -46,22 +44,30 @@
         in_specs=[pl.BlockSpec(memory_space=pltpu.SMEM), pl.BlockSpec(memory_space=pltpu.VMEM)],
         out_specs=pl.BlockSpec(memory_space=pltpu.VMEM),
         scratch_shapes=[pltpu.VMEM((held * pitch, LANES), jnp.float32)],
-        compiler_params=pltpu.CompilerParams(vmem_limit_bytes=32 << 20),
+        compiler_params=pltpu.CompilerParams(vmem_limit_bytes=60 << 20),
         cost_estimate=pl.CostEstimate(flops=10_000_000, bytes_accessed=6 << 20, transcendentals=0),
         name="packed_tiles",
     )(source, tiles)
 
 
-def place_kernel(code_ref, tiles_ref, front_ref, out_ref, sum_ref, *, unroll):
+def place_kernel(code_ref, tiles_ref, front_hbm, out_ref, sum_ref, front_ref, front_sem, *, unroll):
     rows, cols = front_ref.shape
     blocks = cols // LANES
     flips = -(-rows // LANES)
     half_rows = TB * TB // LANES
-    sum_ref[...] = jnp.zeros_like(sum_ref)
+    group, groups = pl.program_id(0), pl.num_programs(0)
+    count = tiles_ref.shape[0]
+    front_copy = pltpu.make_async_copy(front_hbm, front_ref, front_sem)
+
+    @pl.when(group == 0)
+    def _():
+        front_copy.start()
+        sum_ref[...] = jnp.zeros_like(sum_ref)
+
     left = lax.broadcasted_iota(jnp.int32, (half_rows, LANES), 1) < TB
 
     def step(q, carry):
-        code = code_ref[q]
+        code = code_ref[group * count + q]
         start = pl.multiple_of((code // 2) * TB, TB)
         odd = code % 2
         tile = tiles_ref[q]
@@ -76,15 +82,18 @@
         sum_ref[uneven, :] = sum_ref[uneven, :] + lower
         return carry
 
-    lax.fori_loop(0, tiles_ref.shape[0], step, 0, unroll=unroll)
-    for block in range(blocks):
-        lo, hi = block * LANES, (block + 1) * LANES
-        out_ref[:, lo:hi] = front_ref[:, lo:hi] + sum_ref[block * rows : (block + 1) * rows, :]
-        for flip in range(flips):
-            at = blocks * rows + flip * cols + lo
-            size = min(LANES, rows - flip * LANES)
-            span = slice(flip * LANES, flip * LANES + size)
-            out_ref[span, lo:hi] = out_ref[span, lo:hi] + sum_ref[at : at + LANES, :].T[:size, :]
+    lax.fori_loop(0, count, step, 0, unroll=unroll)
+    @pl.when(group == groups - 1)
+    def _():
+        front_copy.wait()
+        for block in range(blocks):
+            lo, hi = block * LANES, (block + 1) * LANES
+            out_ref[:, lo:hi] = front_ref[:, lo:hi] + sum_ref[block * rows : (block + 1) * rows, :]
+            for flip in range(flips):
+                at = blocks * rows + flip * cols + lo
+                size = min(LANES, rows - flip * LANES)
+                span = slice(flip * LANES, flip * LANES + size)
+                out_ref[span, lo:hi] = out_ref[span, lo:hi] + sum_ref[at : at + LANES, :].T[:size, :]
 
 
 def placed(front, tiles, code):
@@ -93,10 +102,19 @@
     return pl.pallas_call(
         functools.partial(place_kernel, unroll=8),
         out_shape=jax.ShapeDtypeStruct(front.shape, jnp.float32),
-        in_specs=[pl.BlockSpec(memory_space=pltpu.SMEM)] + [pl.BlockSpec(memory_space=pltpu.VMEM)] * 2,
-        out_specs=pl.BlockSpec(memory_space=pltpu.VMEM),
-        scratch_shapes=[pltpu.VMEM((total, LANES), jnp.float32)],
-        compiler_params=pltpu.CompilerParams(vmem_limit_bytes=32 << 20),
+        grid=(tiles.shape[0] // GROUP,),
+        in_specs=[
+            pl.BlockSpec(memory_space=pltpu.SMEM),
+            pl.BlockSpec((GROUP, *tiles.shape[1:]), lambda g: (g, 0, 0)),
+            pl.BlockSpec(memory_space=pltpu.HBM),
+        ],
+        out_specs=pl.BlockSpec(front.shape, lambda g: (0, 0)),
+        scratch_shapes=[
+            pltpu.VMEM((total, LANES), jnp.float32),
+            pltpu.VMEM(front.shape, jnp.float32),
+            pltpu.SemaphoreType.DMA,
+        ],
+        compiler_params=pltpu.CompilerParams(vmem_limit_bytes=60 << 20),
         cost_estimate=pl.CostEstimate(flops=10_000_000, bytes_accessed=10 << 20, transcendentals=0),
         name="placed_tiles",
     )(code, tiles, front)
@@ -107,7 +125,7 @@
 
 def exchange_kernel(
     tiles_ref, code_ref, probe_ref, tiles_in, code_in, probe_rows,
-    tiles_send, tiles_recv, code_send, code_recv, probe_send, probe_recv,
+    tiles_send, tiles_recv, code_send, code_recv, probe_send, probe_recv, own_sem,
 ):
     n_row, n_col = lax.axis_size("row"), lax.axis_size("col")
     devices = n_row * n_col
@@ -157,13 +175,15 @@
     def _():
         probe_rows[...] = probe_ref[at, :]
 
-    tiles_in[me] = tiles_ref[me]
+    own = pltpu.make_async_copy(tiles_ref.at[me], tiles_in.at[me], own_sem)
+    own.start()
     code_in[me] = code_ref[me]
     others = pl.ds(0, devices - 1)
 
     def all_of(ref, sem):
         pltpu.make_async_copy(ref.at[others], ref.at[others], sem).wait()
 
+    own.wait()
     all_of(code_in, code_recv)
     all_of(tiles_in, tiles_recv)
     all_of(code_ref, code_send)
@@ -187,16 +207,17 @@
             jax.ShapeDtypeStruct(code.shape, jnp.int32),
             jax.ShapeDtypeStruct((rows, probe.shape[1]), jnp.float32),
         ),
-        in_specs=[pl.BlockSpec(memory_space=pltpu.VMEM)] * 3,
-        out_specs=[pl.BlockSpec(memory_space=pltpu.VMEM)] * 3,
-        scratch_shapes=[dma] * 6,
-        compiler_params=pltpu.CompilerParams(has_side_effects=True, vmem_limit_bytes=32 << 20),
+        in_specs=[pl.BlockSpec(memory_space=pltpu.HBM)] + [pl.BlockSpec(memory_space=pltpu.VMEM)] * 2,
+        out_specs=[pl.BlockSpec(memory_space=pltpu.HBM)] + [pl.BlockSpec(memory_space=pltpu.VMEM)] * 2,
+        scratch_shapes=[dma] * 7,
+        compiler_params=pltpu.CompilerParams(has_side_effects=True, vmem_limit_bytes=60 << 20),
         cost_estimate=pl.CostEstimate(flops=1_000_000_000, bytes_accessed=16 << 20, transcendentals=0),
         name="exchanged_tiles",
     )(tiles, code, probe)
 
 
 def factor_rows(rows, base):
+    groups = len(rows)
     sub = lax.broadcasted_iota(jnp.int32, (8, BLK), 0)
     lane = lax.broadcasted_iota(jnp.int32, (8, BLK), 1)
 
@@ -204,24 +225,24 @@
         here = jnp.where(lane == base + i, rows[g][:, :BLK], 0.0)
         return jnp.broadcast_to(jnp.sum(here, axis=1, keepdims=True), (8, BLK))
 
-    spread = [[column(g, i) if i < 8 * g + 8 else None for i in range(SUB)] for g in range(2)]
+    spread = [[column(g, i) if i < 8 * g + 8 else None for i in range(SUB)] for g in range(groups)]
     halves = [[row[:, :BLK], row[:, BLK:]] for row in rows]
     for i in range(SUB):
         own, at = divmod(i, 8)
         pivot = jnp.broadcast_to(spread[own][i][at : at + 1, :], (8, BLK))
         scale = lax.rsqrt(pivot)
-        lows = [None, None]
-        for g in range(own, 2):
+        lows = [None] * groups
+        for g in range(own, groups):
             low = spread[g][i] * scale
             lows[g] = jnp.where(sub > at, low, 0.0) if g == own else low
         for j in range(i + 1, SUB):
             g_j, at_j = divmod(j, 8)
             factor = jnp.broadcast_to(lows[g_j][at_j : at_j + 1, :], (8, BLK))
-            for g in range(g_j, 2):
+            for g in range(g_j, groups):
                 spread[g][j] = spread[g][j] - lows[g] * factor
         for h in range(2):
             line = jnp.broadcast_to(halves[own][h][at : at + 1, :], (8, BLK)) * scale
-            for g in range(own, 2):
+            for g in range(own, groups):
                 new = halves[g][h] - lows[g] * line
                 halves[g][h] = jnp.where(sub == at, line, new) if g == own else new
     return [jnp.concatenate(half, axis=1) for half in halves]
@@ -232,22 +253,17 @@
 
     def step(s, carry):
         base = pl.multiple_of(s * SUB, SUB)
-        rows = factor_rows([x_ref[pl.ds(base, 8), :], x_ref[pl.ds(base + 8, 8), :]], base)
+        lines = [pl.ds(base + g, 8) for g in range(0, SUB, 8)]
+        rows = factor_rows([x_ref[line, :] for line in lines], base)
         beside(s)
-        x_ref[pl.ds(base, 8), :] = rows[0]
-        x_ref[pl.ds(base + 8, 8), :] = rows[1]
+        for line, value in zip(lines, rows):
+            x_ref[line, :] = value
         done = jnp.concatenate(rows, axis=0)
-        gone = plain_dot(done[:, :BLK].T, done)
+        gone = joined_dot(done[:, :BLK].T, done)
         x_ref[...] = x_ref[...] - jnp.where(row >= base + SUB, gone, 0.0)
         return carry
 
     lax.fori_loop(0, BLK // SUB, step, 0)
-
-
-def plain_dot(a, b):
-    return lax.dot_general(
-        a, b, (((1,), (0,)), ((), ())), precision=HIGH, preferred_element_type=jnp.float32
-    )
 
 
 def halves_of(a):
@@ -255,19 +271,40 @@
     return top, (a - top.astype(jnp.float32)).astype(jnp.bfloat16)
 
 
-def turned_dot(a, b):
+def split_dot(a, b, b_dim):
     a_top, a_rest = halves_of(a)
     b_top, b_rest = halves_of(b)
 
     def part(p, q):
-        return lax.dot_general(p, q, (((1,), (1,)), ((), ())), preferred_element_type=jnp.float32)
+        return lax.dot_general(
+            p, q, (((1,), (b_dim,)), ((), ())), preferred_element_type=jnp.float32
+        )
 
     return part(a_top, b_top) + (part(a_top, b_rest) + part(a_rest, b_top))
 
 
+def plain_dot(a, b):
+    return split_dot(a, b, 0)
+
+
+def turned_dot(a, b):
+    return split_dot(a, b, 1)
+
+
+def joined_dot(a, b):
+    a_top, a_rest = halves_of(a)
+    b_top, b_rest = halves_of(b)
+    return lax.dot_general(
+        jnp.concatenate([a_top, a_top, a_rest], axis=1),
+        jnp.concatenate([b_top, b_rest, b_top], axis=0),
+        (((1,), (0,)), ((), ())),
+        preferred_element_type=jnp.float32,
+    )
+
+
 def panel_kernel(
-    matrix_ref, z_ref, y_ref, panel_ref, y_own_ref, share_ref,
-    w_ref, solved_ref, z_all_ref, fix_ref, m_ref, stage_ref, x_ref, z_in, y_in,
+    matrix_ref, probe_ref, probe_rows_ref, panel_ref, y_own_ref, share_ref,
+    z_ref, y_ref, w_ref, solved_ref, z_all_ref, fix_ref, m_ref, stage_ref, x_ref, z_in, y_in,
     first_send, first_recv, next_send, d_recv, z_send, z_recv, zall_send, zall_recv,
     y_send, y_recv, s_send, s_recv, fix_send, fix_recv,
 ):
@@ -390,7 +427,27 @@
             at = b * BLK + mine * piece - mine * rows
             m_ref[b, own_lines, b * BLK : order] = matrix_ref[at : at + piece, b * BLK : order]
 
-    each(n_col, lambda s: y_copy(s).start())
+    def z_slab(s):
+        lanes = pl.ds(pl.multiple_of(s * z_slab_width, BLK), z_slab_width)
+        line = me_row * rows + lax.broadcasted_iota(jnp.int32, (rows, z_slab_width), 0)
+        chosen = jnp.where(line >= order, probe_rows_ref[:, lanes], 0.0)
+        z_ref[lanes, :] = plain_dot(chosen.T, matrix_ref[:, :order])
+
+    def y_slab(s, first):
+        lanes = pl.ds(pl.multiple_of(s * z_slab_width, BLK), z_slab_width)
+        y_ref[lanes, :] = turned_dot(probe_ref[first:, lanes].T, matrix_ref[:, first:])
+
+    steps = BLK // SUB
+    z_slab_width = z_ref.shape[0] // steps
+
+    @pl.when(me_col != 0)
+    def _():
+        def step(s, carry):
+            y_slab(s, 0)
+            return carry
+
+        lax.fori_loop(0, steps, step, 0)
+        each(n_col, lambda s: y_copy(s).start())
 
     def sum_z():
         own = pl.ds(pl.multiple_of(me_row * z_lines, 8), z_lines)
@@ -431,6 +488,14 @@
             line = me_row * rows + s * slab + lax.broadcasted_iota(jnp.int32, (slab, BLK), 0)
             part = jnp.where(line >= i * BLK // NB * NB, part, 0.0)
         solved_ref[i, lines, :] = part
+
+    def beside(i, s):
+        if i == 0:
+            z_slab(s)
+        else:
+            solve_slab(i - 1, s)
+        if i == 1:
+            y_slab(s, order)
 
     @pl.when(on_panel)
     def _():
@@ -449,7 +514,9 @@
             x_ref[:, BLK:] = eye
             if hi < order:
                 m_ref[i, :, hi:] = own_row[:, BLK:]
-            inverse_factor(x_ref, (lambda s: solve_slab(i - 1, s)) if i else (lambda s: None))
+            inverse_factor(x_ref, functools.partial(beside, i))
+            if i == 1:
+                each(n_col, lambda s: y_copy(s).start())
             if i > 1:
                 solved_copy(i - 1).start()
             if i == 4:
@@ -519,9 +586,9 @@
                 arrived(pieces_of(b, count), first_send.at[b])
 
 
-def panel_parts(matrix, z_part, y_part, order, n_row, n_col):
-    lines_z, lines_y = z_part.shape[0] // n_row, y_part.shape[0] // n_col
-    rows = matrix.shape[0]
+def panel_parts(matrix, probe, probe_rows, order, n_row, n_col):
+    rows, columns = matrix.shape[0], probe.shape[1]
+    lines_z, lines_y = columns // n_row, columns // n_col
     width = order // n_col
     dma = pltpu.SemaphoreType.DMA
     whole = functools.partial(jax.ShapeDtypeStruct, dtype=jnp.float32)
@@ -529,21 +596,23 @@
         panel_kernel,
         out_shape=(
             whole((rows, width)),
-            whole((lines_y, y_part.shape[1])),
-            whole((lines_y, y_part.shape[1])),
+            whole((lines_y, rows)),
+            whole((lines_y, rows)),
         ),
         in_specs=[pl.BlockSpec(memory_space=pltpu.VMEM)] * 3,
         out_specs=[pl.BlockSpec(memory_space=pltpu.VMEM)] * 3,
         scratch_shapes=[
+            pltpu.VMEM((columns, order), jnp.float32),
+            pltpu.VMEM((columns, rows), jnp.float32),
             pltpu.VMEM((order // BLK, BLK, order), jnp.float32),
             pltpu.VMEM((n_col, rows, width), jnp.float32),
-            pltpu.VMEM(z_part.shape, jnp.float32),
-            pltpu.VMEM(y_part.shape, jnp.float32),
+            pltpu.VMEM((columns, order), jnp.float32),
+            pltpu.VMEM((columns, rows), jnp.float32),
             pltpu.VMEM((order // BLK, BLK, order), jnp.float32),
             pltpu.VMEM((order // BLK, BLK // n_row, order), jnp.float32),
             pltpu.VMEM((BLK, 2 * BLK), jnp.float32),
-            pltpu.VMEM((n_row, lines_z, z_part.shape[1]), jnp.float32),
-            pltpu.VMEM((n_col, lines_y, y_part.shape[1]), jnp.float32),
+            pltpu.VMEM((n_row, lines_z, order), jnp.float32),
+            pltpu.VMEM((n_col, lines_y, rows), jnp.float32),
             *[dma((order // BLK,))] * 4,
             *[dma((n_row,))] * 4,
             *[dma((n_col,))] * 3, dma((1,)), dma((n_col,)), dma((1,)),
@@ -551,7 +620,7 @@
         compiler_params=pltpu.CompilerParams(has_side_effects=True, vmem_limit_bytes=60 << 20),
         cost_estimate=pl.CostEstimate(flops=3_000_000_000, bytes_accessed=16 << 20, transcendentals=0),
         name="panel_parts",
-    )(matrix, z_part, y_part)
+    )(matrix, probe, probe_rows)
 
 
 def per_device(front, child_tiles, tile_target, tile_count, probe):
@@ -592,13 +661,7 @@
     matrix = placed(front, incoming.reshape(2 * devices, chunks, LANES), landing[:, 0, :2].reshape(-1))
 
     global_rows = me_row * rows + jnp.arange(rows, dtype=jnp.int32)
-    global_cols = me_col * cols + jnp.arange(cols, dtype=jnp.int32)
-    by_cols = jnp.where((global_cols >= start)[:, None], probe, 0.0)
-    by_rows = jnp.where((global_rows >= start)[:, None], probe_rows, 0.0)
-    y_part = lax.dot_general(by_cols, matrix, (((0,), (1,)), ((), ())), precision=GOOD)
-    panel = matrix[:, :start]
-    z_part = lax.dot_general(by_rows, panel, (((0,), (0,)), ((), ())), precision=GOOD)
-    panel_factor, y_own, fix_own = panel_parts(matrix, z_part, y_part, start, n_row, n_col)
+    panel_factor, y_own, fix_own = panel_parts(matrix, probe, probe_rows, start, n_row, n_col)
     sketch = jnp.where((global_rows >= start)[:, None], (y_own - fix_own).T, 0.0)
     return (panel_factor, sketch)
 

time: 223 us -> 192 us (0.86)
  matrix products: 14.9 us -> 0 us
  local copies, waits for them, and re-layouts: 16.2 us -> 5.69 us
  Pallas kernels: 185 us -> 179 us
    pallas_call x1, Pallas kernels: 115 us -> 98.5 us  [panel_parts(): pl.pallas_call(panel_kernel, out_shape=(whole((rows, width)), whole((line...]
    dot_general x2 -> x0, matrix products: 14.9 us -> none  [the longest x1 8.64 us: per_device(): lax.dot_general(by_cols, matrix, (((0,), (1,)), ((), ())), precision=GOOD)]
    unnamed x19 -> x1, local copies, waits for them, and re-layouts: 14.3 us -> 1.69 us
    pallas_call x1, Pallas kernels: 5.36 us -> 9.56 us  [placed(): pl.pallas_call(functools.partial(place_kernel, unroll=8), out_shape=jax.S...]
    pallas_call x1, Pallas kernels: 63.6 us -> 66.8 us  [exchanged(): pl.pallas_call(exchange_kernel, out_shape=(jax.ShapeDtypeStruct(tiles.sha...]
    pallas_call x1, Pallas kernels: 1.51 us -> 4.57 us  [packed(): pl.pallas_call(functools.partial(pack_kernel, pitch=pitch, unroll=4), out...]
where the time goes in v4:
time: 192 us
  Pallas kernels  179 us (93%)
  other arithmetic  5.86 us (3%)
  local copies, waits for them, and re-layouts  5.69 us (3%)
    pallas_call x1, Pallas kernels, panel_parts(): pl.pallas_call(panel_kernel, out_shape=(whole((rows, width)), whole((line...  98.5 us
    pallas_call x1, Pallas kernels, exchanged(): pl.pallas_call(exchange_kernel, out_shape=(jax.ShapeDtypeStruct(tiles.sha...  66.8 us
    pallas_call x1, Pallas kernels, placed(): pl.pallas_call(functools.partial(place_kernel, unroll=8), out_shape=jax.S...  9.56 us
    pallas_call x1, Pallas kernels, packed(): pl.pallas_call(functools.partial(pack_kernel, pitch=pitch, unroll=4), out...  4.57 us

profile of v4, /device:TPU:9, one launch (start us, length us, event | category | flops | bytes accessed | tf_op | source)
XLA Modules:
  0.0 191.6 jit_solution(18322498747325424685)
XLA Ops:
  0.6 1.5 fusion.6
  2.1 2.6 %fusion.4 = pred[128]{0:T(512)(128)(4,1)S(1)} fusion(s32[]{:T(128)} %bitcast.1, s32[]{:T(128)} %bitcast.2, s32[]{:T(128)} %bitcast.4, s32[]{:T(128)} %bitcast.3), kind=kLoop, calls=%fused_computation.45 | loop fusion | flops 3072 | bytes 144 | tf_op jit(solution)/shard_map/lt | solution.py:636
  4.7 0.7 and_select_fusion.11
  5.4 0.2 convert_reduce_fusion
  5.6 0.7 select_reduce_fusion
  6.3 4.6 %packed_tiles.1 = f32[256,32,128]{2,1,0:T(8,128)} custom-call(s32[256]{0:T(256)} %get-tuple-element.15.source_ref, f32[128,4096]{1,0:T(8,128)} %tiles_ref.1), custom_call_target="tpu_custom_call" | custom-call | flops 10000000 | bytes 6291456 | tf_op jit(solution)/shard_map/packed_tiles/pallas_call | solution.py:41
  10.9 0.1 reshape.406
  11.0 0.7 pad.4.code_ref
  11.7 66.8 %exchanged_tiles.1 = (f32[128,64,128]{2,1,0:T(8,128)}, s32[128,1,128]{2,1,0:T(1,128)}, f32[576,512]{1,0:T(8,128)}) custom-call(f32[128,64,128]{2,1,0:T(8,128)} %bitcast.13, s32[128,1,128]{2,1,0:T(1,128)} %pad.4.code_ref, f32[1152,512]{1,0:T(8,128)} %probe_ref.3), custom_call_target="tpu_custom_call" | custom-call | flops 1000000000 | bytes 16777216 | tf_op jit(solution)/shard_map/exchanged_tiles/pallas_call | solution.py:203
  78.5 1.0 slice_reduce_fusion
  79.5 0.7 reshape_squeeze.3.code_ref
  80.2 9.6 %placed_tiles.1.matrix_ref = f32[576,1152]{1,0:T(8,128)} custom-call(s32[256]{0:T(256)} %reshape_squeeze.3.code_ref, f32[256,32,128]{2,1,0:T(8,128)} %bitcast.14, f32[576,1152]{1,0:T(8,128)} %front_hbm.1), custom_call_target="tpu_custom_call" | custom-call | flops 10000000 | bytes 10485760 | tf_op jit(solution)/shard_map/placed_tiles/pallas_call | solution.py:102
  89.8 98.5 %panel_parts.1 = (f32[576,128]{1,0:T(8,128)}, f32[64,576]{1,0:T(8,128)}, f32[64,576]{1,0:T(8,128)}) custom-call(f32[576,1152]{1,0:T(8,128)} %placed_tiles.1.matrix_ref, f32[1152,512]{1,0:T(8,128)} %probe_ref.3, f32[576,512]{1,0:T(8,128)} %get-tuple-element.10.probe_rows_ref), custom_call_target="tpu_custom_call" | custom-call | flops 3000000000 | bytes 16777216 | tf_op jit(solution)/shard_map/panel_parts/pallas_call | solution.py:595
  188.3 1.7 select_bitcast_fusion
  189.9 1.7 copy.10
  (3 shorter events, 0.1 us)

commit v5 on v4

--- a/solution.py
+++ b/solution.py
@@ -306,7 +306,7 @@
     matrix_ref, probe_ref, probe_rows_ref, panel_ref, y_own_ref, share_ref,
     z_ref, y_ref, w_ref, solved_ref, z_all_ref, fix_ref, m_ref, stage_ref, x_ref, z_in, y_in,
     first_send, first_recv, next_send, d_recv, z_send, z_recv, zall_send, zall_recv,
-    y_send, y_recv, s_send, s_recv, fix_send, fix_recv,
+    y_send, y_recv, s_send, s_recv, fix_send, fix_recv, ready_sem,
 ):
     me_row, me_col = lax.axis_index("row"), lax.axis_index("col")
     n_row, n_col = z_in.shape[0], y_in.shape[0]
@@ -391,6 +391,33 @@
 
         lax.fori_loop(1, count, step, 0)
 
+    entry = pltpu.get_barrier_semaphore()
+
+    def greet_row(s):
+        pl.semaphore_signal(
+            entry, inc=1, device_id=(me_row, lax.rem(me_col + s, n_col)), device_id_type=MESH
+        )
+
+    @pl.when(on_panel)
+    def _():
+        each(n_row, lambda s: pl.semaphore_signal(
+            entry, inc=1, device_id=(partner(s), me_col), device_id_type=MESH
+        ))
+        each(n_col, greet_row)
+        pl.semaphore_wait(entry, n_row - 1)
+
+    @pl.when(me_col != 0)
+    def _():
+        def greet(s, carry):
+            @pl.when(lax.rem(me_col + s, n_col) != 0)
+            def _():
+                greet_row(s)
+            return carry
+
+        lax.fori_loop(1, n_col, greet, 0)
+        pl.semaphore_wait(entry, n_col - 1)
+        pl.semaphore_signal(ready_sem, inc=1, device_id=(me_row, 0), device_id_type=MESH)
+
     n_roots = -(-order // rows)
     sent = [[] for _ in range(n_roots)]
     for root in range(n_roots):
@@ -408,6 +435,27 @@
                     if to != root:
                         first_copy(b, to, root).start()
 
+    def z_slab(s):
+        lanes = pl.ds(pl.multiple_of(s * z_slab_width, BLK), z_slab_width)
+        line = me_row * rows + lax.broadcasted_iota(jnp.int32, (rows, z_slab_width), 0)
+        chosen = jnp.where(line >= order, probe_rows_ref[:, lanes], 0.0)
+        z_ref[lanes, :] = plain_dot(chosen.T, matrix_ref[:, :order])
+
+    def y_slab(s, first):
+        lanes = pl.ds(pl.multiple_of(s * z_slab_width, BLK), z_slab_width)
+        y_ref[lanes, :] = turned_dot(probe_ref[first:, lanes].T, matrix_ref[:, first:])
+
+    steps = BLK // SUB
+    z_slab_width = z_ref.shape[0] // steps
+
+    @pl.when(on_panel)
+    def _():
+        def step(s, carry):
+            z_slab(s)
+            return carry
+
+        lax.fori_loop(0, steps, step, 0)
+
     local = [[b for b, first, last in sent[root] if first <= root < last] for root in range(n_roots)]
     for b in range(blocks):
         mine = None
@@ -426,19 +474,6 @@
             each(n_row, lambda s: next_copy(b, s, mine).start())
             at = b * BLK + mine * piece - mine * rows
             m_ref[b, own_lines, b * BLK : order] = matrix_ref[at : at + piece, b * BLK : order]
-
-    def z_slab(s):
-        lanes = pl.ds(pl.multiple_of(s * z_slab_width, BLK), z_slab_width)
-        line = me_row * rows + lax.broadcasted_iota(jnp.int32, (rows, z_slab_width), 0)
-        chosen = jnp.where(line >= order, probe_rows_ref[:, lanes], 0.0)
-        z_ref[lanes, :] = plain_dot(chosen.T, matrix_ref[:, :order])
-
-    def y_slab(s, first):
-        lanes = pl.ds(pl.multiple_of(s * z_slab_width, BLK), z_slab_width)
-        y_ref[lanes, :] = turned_dot(probe_ref[first:, lanes].T, matrix_ref[:, first:])
-
-    steps = BLK // SUB
-    z_slab_width = z_ref.shape[0] // steps
 
     @pl.when(me_col != 0)
     def _():
@@ -490,20 +525,17 @@
         solved_ref[i, lines, :] = part
 
     def beside(i, s):
-        if i == 0:
-            z_slab(s)
+        if i:
+            solve_slab(i - 1, s)
         else:
-            solve_slab(i - 1, s)
-        if i == 1:
             y_slab(s, order)
 
     @pl.when(on_panel)
     def _():
+        each(n_row, lambda s: z_copy(s).start())
         for i in range(blocks):
             lo, hi = i * BLK, (i + 1) * BLK
             arrived(pieces_of(i, n_row - 1), d_recv.at[i])
-            if i == 1:
-                each(n_row, lambda s: z_copy(s).start())
             own_row = m_ref[i, :, lo:]
             if i:
                 left = jnp.concatenate([m_ref[b, :, lo:hi].T for b in range(i)], axis=1)
@@ -516,10 +548,11 @@
                 m_ref[i, :, hi:] = own_row[:, BLK:]
             inverse_factor(x_ref, functools.partial(beside, i))
             if i == 1:
+                pl.semaphore_wait(ready_sem, n_col - 1)
                 each(n_col, lambda s: y_copy(s).start())
             if i > 1:
                 solved_copy(i - 1).start()
-            if i == 4:
+            if i == 3:
                 sum_z()
             w_diag = x_ref[:, BLK:]
             w_ref[i, :, lo:hi] = w_diag
@@ -528,7 +561,7 @@
             if hi < order:
                 m_ref[i, :, hi:] = plain_dot(w_diag, m_ref[i, :, hi:])
                 w_ref[i, :, hi:] = jnp.zeros((BLK, order - hi), jnp.float32)
-            if i == 4:
+            if i == 3:
                 each(n_row, lambda s: z_all_copy(s).start())
 
         def last(s, carry):
@@ -615,9 +648,11 @@
             pltpu.VMEM((n_col, lines_y, rows), jnp.float32),
             *[dma((order // BLK,))] * 4,
             *[dma((n_row,))] * 4,
-            *[dma((n_col,))] * 3, dma((1,)), dma((n_col,)), dma((1,)),
+            *[dma((n_col,))] * 3, dma((1,)), dma((n_col,)), dma((1,)), pltpu.SemaphoreType.REGULAR,
         ],
-        compiler_params=pltpu.CompilerParams(has_side_effects=True, vmem_limit_bytes=60 << 20),
+        compiler_params=pltpu.CompilerParams(
+            has_side_effects=True, vmem_limit_bytes=60 << 20, collective_id=1
+        ),
         cost_estimate=pl.CostEstimate(flops=3_000_000_000, bytes_accessed=16 << 20, transcendentals=0),
         name="panel_parts",
     )(matrix, probe, probe_rows)

time: 192 us -> 194 us (1.010)
  Pallas kernels: 179 us -> 181 us
where the time goes in v5:
time: 194 us; the launch traced here: 193 us
  Pallas kernels  181 us (93%)
  other arithmetic  5.86 us (3%)
  local copies, waits for them, and re-layouts  5.69 us (3%)
    pallas_call x1, Pallas kernels, panel_parts(): pl.pallas_call(panel_kernel, out_shape=(whole((rows, width)), whole((line...  99.8 us
    pallas_call x1, Pallas kernels, exchanged(): pl.pallas_call(exchange_kernel, out_shape=(jax.ShapeDtypeStruct(tiles.sha...  66.8 us
    pallas_call x1, Pallas kernels, placed(): pl.pallas_call(functools.partial(place_kernel, unroll=8), out_shape=jax.S...  9.55 us
    pallas_call x1, Pallas kernels, packed(): pl.pallas_call(functools.partial(pack_kernel, pitch=pitch, unroll=4), out...  4.57 us

profile of v5, /device:TPU:9, one launch (start us, length us, event | category | flops | bytes accessed | tf_op | source)
XLA Modules:
  0.0 192.9 jit_solution(16719864627427459559)
XLA Ops:
  0.6 1.5 fusion.6
  2.1 2.6 %fusion.4 = pred[128]{0:T(512)(128)(4,1)S(1)} fusion(s32[]{:T(128)} %bitcast.1, s32[]{:T(128)} %bitcast.2, s32[]{:T(128)} %bitcast.4, s32[]{:T(128)} %bitcast.3), kind=kLoop, calls=%fused_computation.45 | loop fusion | flops 3072 | bytes 144 | tf_op jit(solution)/shard_map/lt | solution.py:671
  4.7 0.7 and_select_fusion.11
  5.4 0.2 convert_reduce_fusion
  5.6 0.7 select_reduce_fusion
  6.3 4.6 %packed_tiles.1 = f32[256,32,128]{2,1,0:T(8,128)} custom-call(s32[256]{0:T(256)} %get-tuple-element.15.source_ref, f32[128,4096]{1,0:T(8,128)} %tiles_ref.1), custom_call_target="tpu_custom_call" | custom-call | flops 10000000 | bytes 6291456 | tf_op jit(solution)/shard_map/packed_tiles/pallas_call | solution.py:41
  10.9 0.1 reshape.406
  11.0 0.7 pad.4.code_ref
  11.7 66.8 %exchanged_tiles.1 = (f32[128,64,128]{2,1,0:T(8,128)}, s32[128,1,128]{2,1,0:T(1,128)}, f32[576,512]{1,0:T(8,128)}) custom-call(f32[128,64,128]{2,1,0:T(8,128)} %bitcast.13, s32[128,1,128]{2,1,0:T(1,128)} %pad.4.code_ref, f32[1152,512]{1,0:T(8,128)} %probe_ref.3), custom_call_target="tpu_custom_call" | custom-call | flops 1000000000 | bytes 16777216 | tf_op jit(solution)/shard_map/exchanged_tiles/pallas_call | solution.py:203
  78.5 1.0 slice_reduce_fusion
  79.5 0.7 reshape_squeeze.3.code_ref
  80.2 9.6 %placed_tiles.1.matrix_ref = f32[576,1152]{1,0:T(8,128)} custom-call(s32[256]{0:T(256)} %reshape_squeeze.3.code_ref, f32[256,32,128]{2,1,0:T(8,128)} %bitcast.14, f32[576,1152]{1,0:T(8,128)} %front_hbm.1), custom_call_target="tpu_custom_call" | custom-call | flops 10000000 | bytes 10485760 | tf_op jit(solution)/shard_map/placed_tiles/pallas_call | solution.py:102
  89.7 99.8 %panel_parts.1 = (f32[576,128]{1,0:T(8,128)}, f32[64,576]{1,0:T(8,128)}, f32[64,576]{1,0:T(8,128)}) custom-call(f32[576,1152]{1,0:T(8,128)} %placed_tiles.1.matrix_ref, f32[1152,512]{1,0:T(8,128)} %probe_ref.3, f32[576,512]{1,0:T(8,128)} %get-tuple-element.10.probe_rows_ref), custom_call_target="tpu_custom_call" | custom-call | flops 3000000000 | bytes 16777216 | tf_op jit(solution)/shard_map/panel_parts/pallas_call | solution.py:628
  189.5 1.7 select_bitcast_fusion
  191.2 1.7 copy.10
  (3 shorter events, 0.1 us)

commit v6 on v4

--- a/solution.py
+++ b/solution.py
@@ -551,15 +551,19 @@
 
         each(n_row, wait_all)
         inverse = w_ref[...].reshape(order, order)
-        weights = turned_dot(z_all_ref[...], inverse)
+        pair = 2 * BLK
+        weights = jnp.concatenate(
+            [
+                turned_dot(z_all_ref[:, : p + pair], inverse[p : p + pair, : p + pair])
+                for p in range(0, order, pair)
+            ],
+            axis=1,
+        )
+        wide = jnp.concatenate([solved_ref[i] for i in range(blocks)], axis=1)
         half = fix_ref.shape[0] // 2
         for part in (1, 0):
             lines = slice(part * half, (part + 1) * half)
-            total = None
-            for i in range(blocks):
-                term = turned_dot(weights[lines, i * BLK : (i + 1) * BLK], solved_ref[i])
-                total = term if total is None else total + term
-            fix_ref[lines, :] = total
+            fix_ref[lines, :] = turned_dot(weights[lines, :], wide)
             for to in range(part * n_col // 2, (part + 1) * n_col // 2):
                 if to:
                     fix_copy(to).start()

time: 192 us -> 189 us (0.984)
  Pallas kernels: 179 us -> 176 us
    pallas_call x1, Pallas kernels: 98.5 us -> 95.1 us  [panel_parts(): pl.pallas_call(panel_kernel, out_shape=(whole((rows, width)), whole((line...]
where the time goes in v6:
time: 189 us; the launch traced here: 188 us
  Pallas kernels  176 us (93%)
  other arithmetic  5.86 us (3%)
  local copies, waits for them, and re-layouts  5.69 us (3%)
    pallas_call x1, Pallas kernels, panel_parts(): pl.pallas_call(panel_kernel, out_shape=(whole((rows, width)), whole((line...  95.1 us
    pallas_call x1, Pallas kernels, exchanged(): pl.pallas_call(exchange_kernel, out_shape=(jax.ShapeDtypeStruct(tiles.sha...  66.8 us
    pallas_call x1, Pallas kernels, placed(): pl.pallas_call(functools.partial(place_kernel, unroll=8), out_shape=jax.S...  9.55 us
    pallas_call x1, Pallas kernels, packed(): pl.pallas_call(functools.partial(pack_kernel, pitch=pitch, unroll=4), out...  4.57 us

profile of v6, /device:TPU:9, one launch (start us, length us, event | category | flops | bytes accessed | tf_op | source)
XLA Modules:
  0.0 188.2 jit_solution(15427587491347697751)
XLA Ops:
  0.6 1.5 fusion.6
  2.1 2.6 %fusion.4 = pred[128]{0:T(512)(128)(4,1)S(1)} fusion(s32[]{:T(128)} %bitcast.1, s32[]{:T(128)} %bitcast.2, s32[]{:T(128)} %bitcast.4, s32[]{:T(128)} %bitcast.3), kind=kLoop, calls=%fused_computation.45 | loop fusion | flops 3072 | bytes 144 | tf_op jit(solution)/shard_map/lt | solution.py:640
  4.7 0.7 and_select_fusion.11
  5.4 0.2 convert_reduce_fusion
  5.6 0.7 select_reduce_fusion
  6.3 4.6 %packed_tiles.1 = f32[256,32,128]{2,1,0:T(8,128)} custom-call(s32[256]{0:T(256)} %get-tuple-element.15.source_ref, f32[128,4096]{1,0:T(8,128)} %tiles_ref.1), custom_call_target="tpu_custom_call" | custom-call | flops 10000000 | bytes 6291456 | tf_op jit(solution)/shard_map/packed_tiles/pallas_call | solution.py:41
  10.9 0.1 reshape.406
  11.0 0.7 pad.4.code_ref
  11.7 66.8 %exchanged_tiles.1 = (f32[128,64,128]{2,1,0:T(8,128)}, s32[128,1,128]{2,1,0:T(1,128)}, f32[576,512]{1,0:T(8,128)}) custom-call(f32[128,64,128]{2,1,0:T(8,128)} %bitcast.13, s32[128,1,128]{2,1,0:T(1,128)} %pad.4.code_ref, f32[1152,512]{1,0:T(8,128)} %probe_ref.3), custom_call_target="tpu_custom_call" | custom-call | flops 1000000000 | bytes 16777216 | tf_op jit(solution)/shard_map/exchanged_tiles/pallas_call | solution.py:203
  78.5 1.0 slice_reduce_fusion
  79.5 0.7 reshape_squeeze.3.code_ref
  80.2 9.6 %placed_tiles.1.matrix_ref = f32[576,1152]{1,0:T(8,128)} custom-call(s32[256]{0:T(256)} %reshape_squeeze.3.code_ref, f32[256,32,128]{2,1,0:T(8,128)} %bitcast.14, f32[576,1152]{1,0:T(8,128)} %front_hbm.1), custom_call_target="tpu_custom_call" | custom-call | flops 10000000 | bytes 10485760 | tf_op jit(solution)/shard_map/placed_tiles/pallas_call | solution.py:102
  89.7 95.1 %panel_parts.1 = (f32[576,128]{1,0:T(8,128)}, f32[64,576]{1,0:T(8,128)}, f32[64,576]{1,0:T(8,128)}) custom-call(f32[576,1152]{1,0:T(8,128)} %placed_tiles.1.matrix_ref, f32[1152,512]{1,0:T(8,128)} %probe_ref.3, f32[576,512]{1,0:T(8,128)} %get-tuple-element.10.probe_rows_ref), custom_call_target="tpu_custom_call" | custom-call | flops 3000000000 | bytes 16777216 | tf_op jit(solution)/shard_map/panel_parts/pallas_call | solution.py:599
  184.8 1.7 select_bitcast_fusion
  186.5 1.7 copy.10
  (3 shorter events, 0.1 us)
